TPU v7x, 32 devices: a whole 2x2x4 slice. The times are simulated.
32 devices in a mesh: lat: 4 (over z), lon: 8 (over y, x, core).
Axes of the slice: x: 2, y: 2, z: 4, core: 2. Of those that a mesh axis runs over, the one named last changes fastest.
Arguments:
- inputs: bfloat16 [4, 32, 256, 800], P(None, 'lat', 'lon'), may hold values from -6 to 6
- conv_kernel: bfloat16 [7, 7, 800], replicated, may hold values from -0.875 to 0.875
- norm_gain: bfloat16 [800], replicated, may hold values from 0.5 to 1.5
- norm_shift: bfloat16 [800], replicated, may hold values from -3 to 3
- w_in: bfloat16 [800, 3200], replicated, may hold values from -0.21875 to 0.21875
- b_in: bfloat16 [3200], replicated, may hold values from -3 to 3
- w_out: bfloat16 [3200, 800], replicated, may hold values from -0.109375 to 0.109375
- b_out: bfloat16 [800], replicated, may hold values from -3 to 3
- ocean_mask: int32 [32, 256], P('lat', 'lon'), may hold values from 0 to 1, as said below
- lengths: int32 [4], replicated, may hold values from 1 to 8, as said below
- cotangent: bfloat16 [4, 32, 256, 800], P(None, 'lat', 'lon'), may hold values from -6 to 6
Outputs:
- output: bfloat16 [4, 32, 256, 800], P(None, 'lat', 'lon')
- d_inputs: bfloat16 [4, 32, 256, 800], P(None, 'lat', 'lon')
- d_kernel: float32 [7, 7, 800], replicated
- d_gain: float32 [800], replicated
- d_shift: float32 [800], replicated
- d_w_in: float32 [800, 3200], replicated
- d_b_in: float32 [3200], replicated
- d_w_out: float32 [3200, 800], replicated
- d_b_out: float32 [800], replicated
Inputs may be any that keep to these rules, and one draw needn't show every extreme that they name: `ocean_mask`: a 0/1 mask; the last latitude row is all ocean. `lengths`: some micro-batch completes the whole rollout.
All inputs are finite; a program needn't handle non-finite values.
Results may differ from a plain program's by a relative error of at most 0.0063.
Values may be sent and summed in bfloat16 or wider, within the bound.
A program may use at most 128 MiB of HBM per device.

v0:
```python
import jax
import jax.numpy as jnp
from jax import lax
from jax.sharding import PartitionSpec as P

KS = 7
ROLLOUT = 8


epsilon = 1e-05


def with_halo(value, sides, width):
    for axis, dim in sides:
        count, length = (lax.axis_size(axis), value.shape[dim])
        up = [(i, (i + 1) % count) for i in range(count - 1)]
        down = [(j, i) for i, j in up]
        last = lax.slice_in_dim(value, length - width, length, axis=dim)
        initial = lax.slice_in_dim(value, 0, width, axis=dim)
        before = lax.ppermute(last, axis, up)
        after = lax.ppermute(initial, axis, down)
        value = jnp.concatenate([before, value, after], axis=dim)
    return value


def smooth_gate(values):
    return jax.nn.gelu(values, approximate=True)


def body(
    inputs,
    conv_kernel,
    norm_gain,
    norm_shift,
    w_in,
    b_in,
    w_out,
    b_out,
    ocean_mask,
    lengths,
    cotangent,
):
    batches, tile_rows, tile_cols, channels = inputs.shape
    half_side = KS // 2
    padded = with_halo(inputs, (("lat", 1), ("lon", 2)), half_side).astype(jnp.float32)
    kernel = conv_kernel.astype(jnp.float32)
    convolved = jnp.zeros(inputs.shape, jnp.float32)
    for row_shift in range(KS):
        for col_shift in range(KS):
            convolved = (
                convolved
                + kernel[row_shift, col_shift]
                * padded[:, row_shift : row_shift + tile_rows, col_shift : col_shift + tile_cols]
            )
    ocean_cells = ocean_mask.astype(jnp.float32)[None, :, :, None]
    local_count = jnp.sum(ocean_mask).astype(jnp.float32) * batches
    masked = convolved * ocean_cells
    sum_cells, cell_count = lax.psum((jnp.sum(masked, axis=(0, 1, 2)), local_count), ("lat", "lon"))
    mean_value = sum_cells / cell_count
    centered = convolved - mean_value
    variance = (
        lax.psum(jnp.sum(centered * centered * ocean_cells, axis=(0, 1, 2)), ("lat", "lon"))
        / cell_count
    )
    inv_std = lax.rsqrt(variance + epsilon)
    standard = centered * inv_std
    gain_vec = norm_gain.astype(jnp.float32)
    normed = (
        (standard * gain_vec + norm_shift.astype(jnp.float32))
        .astype(jnp.bfloat16)
        .reshape(-1, channels)
    )
    pre_gate = jnp.dot(normed, w_in, preferred_element_type=jnp.float32) + b_in.astype(jnp.float32)
    activated, gate_back = jax.vjp(smooth_gate, pre_gate)
    act_low = activated.astype(jnp.bfloat16)
    branch = jnp.dot(act_low, w_out, preferred_element_type=jnp.float32) + b_out.astype(jnp.float32)
    output = (inputs.astype(jnp.float32) + ocean_cells * branch.reshape(inputs.shape)).astype(
        jnp.bfloat16
    )
    kept_steps = lengths.astype(jnp.float32) / ROLLOUT
    d_output = cotangent.astype(jnp.float32) * kept_steps[:, None, None, None]
    d_branch = (d_output * ocean_cells).reshape(-1, channels)
    branch_low = d_branch.astype(jnp.bfloat16)
    local_b_out = jnp.sum(d_branch, axis=0)
    local_w_out = lax.dot_general(
        act_low, branch_low, (((0,), (0,)), ((), ())), preferred_element_type=jnp.float32
    )
    d_act = lax.dot_general(
        branch_low, w_out, (((1,), (1,)), ((), ())), preferred_element_type=jnp.float32
    )
    d_pre = gate_back(d_act)[0]
    pre_low = d_pre.astype(jnp.bfloat16)
    local_b_in = jnp.sum(d_pre, axis=0)
    local_w_in = lax.dot_general(
        normed, pre_low, (((0,), (0,)), ((), ())), preferred_element_type=jnp.float32
    )
    d_normed = lax.dot_general(
        pre_low, w_in, (((1,), (1,)), ((), ())), preferred_element_type=jnp.float32
    ).reshape(inputs.shape)
    d_shift, d_gain = lax.psum(
        (jnp.sum(d_normed, axis=(0, 1, 2)), jnp.sum(d_normed * standard, axis=(0, 1, 2))),
        ("lat", "lon"),
    )
    d_conv = (
        gain_vec * inv_std * (d_normed - ocean_cells * (d_shift + standard * d_gain) / cell_count)
    )
    conv_low = d_conv.astype(jnp.bfloat16)
    conv_back = conv_low.astype(jnp.float32)
    d_padded = with_halo(conv_low, (("lat", 1), ("lon", 2)), half_side).astype(jnp.float32)
    d_inputs = d_output
    kernel_rows = []
    for row_shift in range(KS):
        kernel_cols = []
        for col_shift in range(KS):
            top_edge = 2 * half_side - row_shift
            left_edge = 2 * half_side - col_shift
            d_inputs = (
                d_inputs
                + kernel[row_shift, col_shift]
                * d_padded[:, top_edge : top_edge + tile_rows, left_edge : left_edge + tile_cols]
            )
            kernel_cols.append(
                jnp.sum(
                    padded[:, row_shift : row_shift + tile_rows, col_shift : col_shift + tile_cols]
                    * conv_back,
                    axis=(0, 1, 2),
                )
            )
        kernel_rows.append(jnp.stack(kernel_cols, axis=0))
    local_kernel = jnp.stack(kernel_rows, axis=0)
    d_w_in, d_b_in, d_w_out, d_b_out, d_kernel = lax.psum(
        (local_w_in, local_b_in, local_w_out, local_b_out, local_kernel), ("lat", "lon")
    )
    return (
        output,
        d_inputs.astype(jnp.bfloat16),
        d_kernel,
        d_gain,
        d_shift,
        d_w_in,
        d_b_in,
        d_w_out,
        d_b_out,
    )


def solution(mesh):
    in_specs = (
        P(None, "lat", "lon", None),
        P(),
        P(),
        P(),
        P(),
        P(),
        P(),
        P(),
        P("lat", "lon"),
        P(),
        P(None, "lat", "lon", None),
    )
    out_specs = (
        P(None, "lat", "lon", None),
        P(None, "lat", "lon", None),
        P(),
        P(),
        P(),
        P(),
        P(),
        P(),
        P(),
    )
    return jax.shard_map(body, mesh=mesh, in_specs=in_specs, out_specs=out_specs, check_vma=False)
```

profile of v0, /device:TPU:0, one launch (start us, length us, event | category | flops | bytes accessed | tf_op | source)
XLA Modules:
  0.0 802.9 jit_solution(7980554916226600556)
XLA Ops:
  8.8 5.0 collective-permute-start
  18.2 10.2 %collective-permute-done = bf16[4,3,32,800]{3,2,1,0:T(8,128)(2,1)S(1)} collective-permute-done((bf16[4,3,32,800]{3,2,1,0:T(8,128)(2,1)S(1)}, bf16[4,3,32,800]{3,2,1,0:T(8,128)(2,1)S(1)}, u32[]{:S(2)}, u32[]{:S(2)}) %collective-permute-start) | collective-permute-done | bytes 614432 | tf_op jit(solution)/shard_map/ppermute | solution.py:20
  28.9 3.7 collective-permute-done.1
  36.0 3.1 collective-permute-start.2
  41.1 5.5 maximum_convert_fusion
  47.0 83.2 %multiply_reduce_fusion.2 = (f32[800]{0:T(1024)S(1)}, f32[4,8,32,800]{3,2,1,0:T(8,128)}) fusion(f32[8,32]{1,0:T(8,128)S(1)} %get-tuple-element.136, f32[4,14,38,800]{3,2,1,0:T(8,128)} %maximum_convert_fusion, f32[800]{0:T(1024)S(1)} %get-tuple-element.59, f32[800]{0:T(1024)S(1)} %get-tuple-element.60, f32[800]{0:T(1024)S(1)} %get-tuple-element.61, ...), kind=kLoop, calls=%fused_computation.217 | loop fusion | flops 81100000 | bytes 164001024 | tf_op jit(solution)/shard_map/reduce_sum | solution.py:58
  130.2 46.7 %all-reduce.1 = (f32[800]{0:T(1024)S(1)}, f32[]{:T(128)}) all-reduce(f32[800]{0:T(1024)S(1)} %get-tuple-element.123, f32[]{:T(128)S(6)} %mul.1208), channel_id=1, replica_groups=mesh['lat'=4,'lon'=8] {'lat','lon'}, use_global_device_ids=true, to_apply=%region_1.0 | all-reduce | flops 801 | bytes 6408 | tf_op jit(solution)/shard_map/psum | solution.py:58
  177.6 4.4 fusion.106
  182.0 40.3 %psum.72 = f32[800]{0:T(1024)S(1)} all-reduce(f32[800]{0:T(1024)S(1)} %get-tuple-element.108), channel_id=1, replica_groups=mesh['lat'=4,'lon'=8] {'lat','lon'}, use_global_device_ids=true, to_apply=%region_5.0 | all-reduce | flops 800 | bytes 6400 | tf_op jit(solution)/shard_map/psum | solution.py:62
  225.8 13.3 %fusion.119 = f32[1024,3200]{1,0:T(8,128)} fusion(bf16[1024,800]{1,0:T(8,128)(2,1)S(1)} %bitcast.38, bf16[800,3200]{1,0:T(8,128)(2,1)} %param.15), kind=kOutput, calls=%fused_computation.297 | convolution fusion | flops 5242880000 | bytes 19865600 | tf_op jit(solution)/shard_map/dot_general | solution.py:73
  239.1 16.8 %fusion.112 = (f32[3200]{0:T(1024)S(1)}, bf16[1024,3200]{1,0:T(8,128)(2,1)}, bf16[1024,3200]{1,0:T(8,128)(2,1)}) fusion(f32[1024,3200]{1,0:T(8,128)} %fusion.119, f32[3200]{0:T(1024)S(1)} %convert_element_type.71, bf16[1024,800]{1,0:T(8,128)(2,1)S(1)} %bitcast.37, bf16[3200,800]{0,1:T(8,128)(2,1)S(1)} %bitcast.43), kind=kOutput, calls=%fused_computation.291 | convolution fusion | flops 5321520128 | bytes 32998400 | tf_op jit(solution)/shard_map/dot_general | solution.py:88
  255.9 9.1 %fusion.118 = (f32[800]{0:T(1024)S(1)}, f32[1024,800]{0,1:T(8,128)}) fusion(bf16[800,3200]{1,0:T(8,128)(2,1)S(1)} %bitcast.41, bf16[1024,3200]{1,0:T(8,128)(2,1)} %get-tuple-element.122), kind=kOutput, calls=%fused_computation.296 | convolution fusion | flops 5243698176 | bytes 14953600 | tf_op jit(solution)/shard_map/dot_general | solution.py:97
  265.1 4.9 copy.24
  269.9 3.8 multiply_reduce_fusion
  273.7 41.2 %all-reduce = (f32[800]{0:T(1024)S(1)}, f32[800]{0:T(1024)S(1)}, f32[3200]{0:T(1024)}, f32[800]{0:T(1024)}) all-reduce(f32[800]{0:T(1024)S(1)} %multiply_reduce_fusion, f32[800]{0:T(1024)S(1)} %get-tuple-element.137, f32[3200]{0:T(1024)S(1)} %get-tuple-element.121, ...), channel_id=1, replica_groups=mesh['lat'=4,'lon'=8] {'lat','lon'}, use_global_device_ids=true, to_apply=%region_9.0 | all-reduce | flops 5600 | bytes 44800 | tf_op jit(solution)/shard_map/psum | solution.py:100
  314.9 36.2 %fusion.53 = (f32[800]{0:T(1024)S(1)}, f32[800]{0:T(1024)S(1)}, f32[800]{0:T(1024)S(1)}, f32[800]{0:T(1024)S(1)}, f32[800]{0:T(1024)S(1)}, /*index=5*/f32[800]{0...) fusion(f32[4,14,38,800]{3,2,1,0:T(8,128)} %maximum_convert_fusi, ...), kind=kLoop, calls=%fused_computation.107 | loop fusion | flops 37668800 | bytes 67249024 | tf_op jit(solution)/shard_map/reduce_sum | solution.py:123
  351.2 22.8 %fusion.52 = (f32[800]{0:T(1024)S(1)}, f32[800]{0:T(1024)S(1)}, f32[800]{0:T(1024)S(1)}, f32[800]{0:T(1024)S(1)}, f32[800]{0:T(1024)S(1)}, /*index=5*/f32[800]{0...) fusion(bf16[4,8,32,800]{3,2,1,0:T(8,128)(2,1)S(1)} %get-tuple-e, ...), kind=kLoop, calls=%fused_computation.106 | loop fusion | flops 22108000 | bytes 44278400 | tf_op jit(solution)/shard_map/reduce_sum | solution.py:123
  374.0 39.8 %fusion.54 = (f32[800]{0:T(1024)S(1)}, f32[800]{0:T(1024)S(1)}, f32[800]{0:T(1024)S(1)}, f32[800]{0:T(1024)S(1)}, f32[800]{0:T(1024)S(1)}, /*index=5*/f32[800]{0...) fusion(bf16[4,8,32,800]{3,2,1,0:T(8,128)(2,1)S(1)} %get-tuple-e, ...), kind=kLoop, calls=%fused_computation.108 | loop fusion | flops 30296000 | bytes 60678400 | tf_op jit(solution)/shard_map/reduce_sum | solution.py:123
  413.8 12.6 %fusion.108 = f32[800,3200]{1,0:T(8,128)} fusion(bf16[1024,800]{1,0:T(8,128)(2,1)S(1)} %bitcast.39, bf16[1024,3200]{1,0:T(8,128)(2,1)} %get-tuple-element.122), kind=kOutput, calls=%fused_computation.220 | convolution fusion | flops 5242880000 | bytes 18432000 | tf_op jit(solution)/shard_map/dot_general | solution.py:94
  427.0 13.1 %fusion.120 = f32[3200,800]{0,1:T(8,128)} fusion(bf16[1024,3200]{1,0:T(8,128)(2,1)} %get-tuple-element.125, bf16[1024,800]{1,0:T(8,128)(2,1)} %bitcast.36), kind=kOutput, calls=%fused_computation.298 | convolution fusion | flops 5242880000 | bytes 18432000 | tf_op jit(solution)/shard_map/dot_general | solution.py:85
  444.0 4.6 collective-permute-start.4
  448.6 11.0 %convolution_add_fusion = f32[1024,800]{0,1:T(8,128)} fusion(bf16[1024,3200]{1,0:T(8,128)(2,1)} %get-tuple-element.125, bf16[3200,800]{0,1:T(8,128)(2,1)} %param.17, f32[800]{0:T(1024)S(1)} %convert_element_type.73), kind=kOutput, calls=%fused_computation.224 | convolution fusion | flops 5243699200 | bytes 14953600 | tf_op jit(solution)/shard_map/dot_general | solution.py:76
  459.6 4.9 copy.23
  464.5 10.2 %collective-permute-done.5 = bf16[4,3,32,800]{3,2,1,0:T(8,128)(2,1)S(1)} collective-permute-done((bf16[4,3,32,800]{3,2,1,0:T(8,128)(2,1)}, bf16[4,3,32,800]{3,2,1,0:T(8,128)(2,1)S(1)}, u32[]{:S(2)}, u32[]{:S(2)}) %collective-permute-start.5) | collective-permute-done | bytes 614432 | tf_op jit(solution)/shard_map/ppermute | solution.py:21
  474.7 4.0 collective-permute-done.4
  480.4 3.1 collective-permute-start.6
  483.4 3.5 add_convert_fusion
  487.3 4.2 maximum_convert_fusion.1
  491.9 104.8 %fusion.56 = bf16[4,8,32,800]{3,2,1,0:T(8,128)(2,1)} fusion(f32[4,14,38,800]{3,2,1,0:T(8,128)} %maximum_convert_fusion.1, bf16[4,8,32,800]{3,2,1,0:T(8,128)(2,1)} %param.21, f32[4]{0:T(128)} %convert_multiply_fusion.51, f32[800]{0:T(1024)S(1)} %copy-done.11, f32[800]{0:T(1024)S(1)} %copy-done.13, f32[800]{0:T(1024)S(1)} %copy-done.15, ...), kind=kLoop, calls=%fused_computation.111 | loop fusion | flops 82739200 | bytes 163996816 | tf_op jit(solution)/shard_map/convert_element_type | solution.py:136
  596.7 184.3 %all-reduce.5.cloned.1.call-done = (f32[7,7,800]{2,1,0:T(8,128)}, f32[800,3200]{1,0:T(8,128)}, f32[3200,800]{0,1:T(8,128)}) async-done(((f32[7,7,800]{2,1,0:T(8,128)}, f32[800,3200]{1,0:T(8,128)}, f32[3200,800]{0,1:T(8,128)}), (f32[7,7,800]{2,1,0:T(8,128)}, f32[800,3200]{1,0:T(8,128)}, f32[3200,800]{0,1:T(8,128)})) %all-reduce.5.cloned.1.call-update) | async-done | bytes 20636816 | tf_op jit(solution)/shard_map/psum | solution.py:131
  782.9 8.7 %copy.37 = f32[800,3200]{1,0:T(8,128)} copy(f32[800,3200]{1,0:T(8,128)} %get-tuple-element.147) | data formatting | bytes 20480000
  791.6 4.0 copy.38
  (297 shorter events, 22.6 us)
Async XLA Ops:
  7.2 773.9 %all-reduce.5.cloned.1.call-start = ((), (), s32[]{:S(2)}) async-start(), calls=%async_computation | async-start | bytes 41361408 | tf_op jit(solution)/shard_map/psum | solution.py:131
  8.8 19.6 %collective-permute-start = (bf16[4,3,32,800]{3,2,1,0:T(8,128)(2,1)S(1)}, bf16[4,3,32,800]{3,2,1,0:T(8,128)(2,1)S(1)}, u32[]{:S(2)}, u32[]{:S(2)}) collective-permute-start(bf16[4,3,32,800]{3,2,1,0:T(8,128)(2,1)S(1)} %get-tuple-element.134), channel_id=1, source_target_pairs={{0,8},{8,16},{16,24},{1,9},{9,17},{17,25},{2,10},{10,18},{18,26},{... | collective-permute-start | bytes 1843208 | tf_op jit(solution)/shard_map/ppermute | solution.py:20
  13.8 18.8 %collective-permute-start.1 = (bf16[4,3,32,800]{3,2,1,0:T(8,128)(2,1)S(1)}, bf16[4,3,32,800]{3,2,1,0:T(8,128)(2,1)S(1)}, u32[]{:S(2)}, u32[]{:S(2)}) collective-permute-start(bf16[4,3,32,800]{3,2,1,0:T(8,128)(2,1)S(1)} %get-tuple-element.133), channel_id=1, source_target_pairs={{8,0},{16,8},{24,16},{9,1},{17,9},{25,17},{10,2},{18,10},{26,18},{... | collective-permute-start | bytes 1843208 | tf_op jit(solution)/shard_map/ppermute | solution.py:21
  16.2 30.4 %copy-start.8 = (f32[800]{0:T(1024)}, f32[800]{0:T(1024)S(1)}, u32[]{:S(2)}) copy-start(f32[800]{0:T(1024)S(1)} %get-tuple-element.58) | copy-start | bytes 9604
  16.2 30.4 %copy-start.10 = (f32[800]{0:T(1024)}, f32[800]{0:T(1024)S(1)}, u32[]{:S(2)}) copy-start(f32[800]{0:T(1024)S(1)} %get-tuple-element.59) | copy-start | bytes 9604
  16.2 30.4 %copy-start.12 = (f32[800]{0:T(1024)}, f32[800]{0:T(1024)S(1)}, u32[]{:S(2)}) copy-start(f32[800]{0:T(1024)S(1)} %get-tuple-element.60) | copy-start | bytes 9604
  16.2 30.4 %copy-start.14 = (f32[800]{0:T(1024)}, f32[800]{0:T(1024)S(1)}, u32[]{:S(2)}) copy-start(f32[800]{0:T(1024)S(1)} %get-tuple-element.61) | copy-start | bytes 9604
  16.2 30.4 %copy-start.16 = (f32[800]{0:T(1024)}, f32[800]{0:T(1024)S(1)}, u32[]{:S(2)}) copy-start(f32[800]{0:T(1024)S(1)} %get-tuple-element.62) | copy-start | bytes 9604
  16.2 30.4 %copy-start.18 = (f32[800]{0:T(1024)}, f32[800]{0:T(1024)S(1)}, u32[]{:S(2)}) copy-start(f32[800]{0:T(1024)S(1)} %get-tuple-element.63) | copy-start | bytes 9604
  16.3 30.4 %copy-start.20 = (f32[800]{0:T(1024)}, f32[800]{0:T(1024)S(1)}, u32[]{:S(2)}) copy-start(f32[800]{0:T(1024)S(1)} %get-tuple-element.64) | copy-start | bytes 9604
  16.3 30.4 %copy-start.22 = (f32[800]{0:T(1024)}, f32[800]{0:T(1024)S(1)}, u32[]{:S(2)}) copy-start(f32[800]{0:T(1024)S(1)} %get-tuple-element.65) | copy-start | bytes 9604
  16.3 30.4 %copy-start.24 = (f32[800]{0:T(1024)}, f32[800]{0:T(1024)S(1)}, u32[]{:S(2)}) copy-start(f32[800]{0:T(1024)S(1)} %get-tuple-element.66) | copy-start | bytes 9604
  16.3 30.4 %copy-start.26 = (f32[800]{0:T(1024)}, f32[800]{0:T(1024)S(1)}, u32[]{:S(2)}) copy-start(f32[800]{0:T(1024)S(1)} %get-tuple-element.67) | copy-start | bytes 9604
  16.3 30.4 %copy-start.28 = (f32[800]{0:T(1024)}, f32[800]{0:T(1024)S(1)}, u32[]{:S(2)}) copy-start(f32[800]{0:T(1024)S(1)} %get-tuple-element.68) | copy-start | bytes 9604
  16.3 30.4 %copy-start.30 = (f32[800]{0:T(1024)}, f32[800]{0:T(1024)S(1)}, u32[]{:S(2)}) copy-start(f32[800]{0:T(1024)S(1)} %get-tuple-element.69) | copy-start | bytes 9604
  16.3 30.4 %copy-start.32 = (f32[800]{0:T(1024)}, f32[800]{0:T(1024)S(1)}, u32[]{:S(2)}) copy-start(f32[800]{0:T(1024)S(1)} %get-tuple-element.70) | copy-start | bytes 9604
  16.3 30.4 %copy-start.34 = (f32[800]{0:T(1024)}, f32[800]{0:T(1024)S(1)}, u32[]{:S(2)}) copy-start(f32[800]{0:T(1024)S(1)} %get-tuple-element.71) | copy-start | bytes 9604
  16.3 30.4 %copy-start.36 = (f32[800]{0:T(1024)}, f32[800]{0:T(1024)S(1)}, u32[]{:S(2)}) copy-start(f32[800]{0:T(1024)S(1)} %get-tuple-element.72) | copy-start | bytes 9604
  16.3 30.4 %copy-start.38 = (f32[800]{0:T(1024)}, f32[800]{0:T(1024)S(1)}, u32[]{:S(2)}) copy-start(f32[800]{0:T(1024)S(1)} %get-tuple-element.73) | copy-start | bytes 9604
  16.4 30.4 %copy-start.40 = (f32[800]{0:T(1024)}, f32[800]{0:T(1024)S(1)}, u32[]{:S(2)}) copy-start(f32[800]{0:T(1024)S(1)} %get-tuple-element.74) | copy-start | bytes 9604
  16.4 30.4 %copy-start.42 = (f32[800]{0:T(1024)}, f32[800]{0:T(1024)S(1)}, u32[]{:S(2)}) copy-start(f32[800]{0:T(1024)S(1)} %get-tuple-element.75) | copy-start | bytes 9604
  16.4 30.4 %copy-start.44 = (f32[800]{0:T(1024)}, f32[800]{0:T(1024)S(1)}, u32[]{:S(2)}) copy-start(f32[800]{0:T(1024)S(1)} %get-tuple-element.76) | copy-start | bytes 9604
  34.7 6.4 collective-permute-start.3
  36.0 5.1 collective-permute-start.2
  47.0 130.6 %copy-start.2 = (bf16[4,8,32,800]{3,2,1,0:T(8,128)(2,1)S(1)}, bf16[4,8,32,800]{3,2,1,0:T(8,128)(2,1)}, u32[]{:S(2)}) copy-start(bf16[4,8,32,800]{3,2,1,0:T(8,128)(2,1)} %param.21) | copy-start | bytes 4915204
  314.9 36.2 %copy-start.88 = (f32[800]{0:T(1024)}, f32[800]{0:T(1024)S(1)}, u32[]{:S(2)}) copy-start(f32[800]{0:T(1024)S(1)} %get-tuple-element.145) | copy-start | bytes 9604
  314.9 36.2 %copy-start.89 = (f32[800]{0:T(1024)}, f32[800]{0:T(1024)S(1)}, u32[]{:S(2)}) copy-start(f32[800]{0:T(1024)S(1)} %get-tuple-element.146) | copy-start | bytes 9604
  374.0 39.8 %copy-start.6 = (bf16[4,8,32,800]{3,2,1,0:T(8,128)(2,1)S(1)}, bf16[4,8,32,800]{3,2,1,0:T(8,128)(2,1)}, u32[]{:S(2)}) copy-start(bf16[4,8,32,800]{3,2,1,0:T(8,128)(2,1)} %copy-done.5) | copy-start | bytes 4915204
  442.7 32.0 %collective-permute-start.5 = (bf16[4,3,32,800]{3,2,1,0:T(8,128)(2,1)}, bf16[4,3,32,800]{3,2,1,0:T(8,128)(2,1)S(1)}, u32[]{:S(2)}, u32[]{:S(2)}) collective-permute-start(bf16[4,3,32,800]{3,2,1,0:T(8,128)(2,1)} %get-tuple-element.132), channel_id=1, source_target_pairs={{8,0},{16,8},{24,16},{9,1},{17,9},{25,17},{10,2},{18,10},{26,18},{... | collective-permute-start | bytes 1843208 | tf_op jit(solution)/shard_map/ppermute | solution.py:21
  444.0 34.7 %collective-permute-start.4 = (bf16[4,3,32,800]{3,2,1,0:T(8,128)(2,1)}, bf16[4,3,32,800]{3,2,1,0:T(8,128)(2,1)S(1)}, u32[]{:S(2)}, u32[]{:S(2)}) collective-permute-start(bf16[4,3,32,800]{3,2,1,0:T(8,128)(2,1)} %get-tuple-element.131), channel_id=1, source_target_pairs={{0,8},{8,16},{16,24},{1,9},{9,17},{17,25},{2,10},{10,18},{18,26},{... | collective-permute-start | bytes 1843208 | tf_op jit(solution)/shard_map/ppermute | solution.py:20
  479.1 8.2 %collective-permute-start.7 = (bf16[4,14,3,800]{3,2,1,0:T(4,128)(2,1)S(1)}, bf16[4,14,3,800]{3,2,1,0:T(4,128)(2,1)S(1)}, u32[]{:S(2)}, u32[]{:S(2)}) collective-permute-start(bf16[4,14,3,800]{3,2,1,0:T(4,128)(2,1)S(1)} %get-tuple-element.127), channel_id=1, source_target_pairs={{1,0},{2,1},{3,2},{4,3},{5,4},{6,5},{7,6},{9,8},{10,9},{11,10},{12... | collective-permute-start | bytes 806408 | tf_op jit(solution)/shard_map/ppermute | solution.py:21
  480.4 6.9 collective-permute-start.6
  (77 other events, 981.9 us)
Sparse Core Ops, SparseCore 0:
  441.4 339.6 all-reduce.4
where the time goes:
time: 811 us; the launch traced here: 803 us
  other arithmetic  316 us (39%)
  waiting for transfers between devices  213 us (26%)
  blocking collectives  128 us (16%)
  matrix products  75.9 us (9%)
  local copies, waits for them, and re-layouts  32.6 us (4%)
  starting transfers between devices  20.9 us (3%)
  between operations  17.2 us (2%)
    psum x1, waiting for transfers between devices, body(): lax.psum((local_w_in, local_b_in, local_w_out, local_b_out, local_kernel)...  184 us
    convert_element_type x1, other arithmetic, body(): d_inputs.astype(jnp.bfloat16)  105 us
    reduce_sum x3, other arithmetic, body(): jnp.sum(padded[:, row_shift:row_shift + tile_rows, col_shift:col_shift +...  98.8 us
    reduce_sum x1, other arithmetic, body(): jnp.sum(masked, axis=(0, 1, 2))  83.2 us
    psum x1, blocking collectives, body(): lax.psum((jnp.sum(masked, axis=(0, 1, 2)), local_count), ('lat', 'lon'))  46.7 us
    psum x1, blocking collectives, body(): lax.psum((jnp.sum(d_normed, axis=(0, 1, 2)), jnp.sum(d_normed * standard,...  41.2 us
    psum x1, blocking collectives, body(): lax.psum(jnp.sum(centered * centered * ocean_cells, axis=(0, 1, 2)), ('la...  40.3 us
    unnamed x211, local copies, waits for them, and re-layouts  17.7 us
  transfers between devices with their start and end apart: 9, of which 5 were waited for; matrix products, arithmetic and copies ran while one was open for 17% of the time, Pallas kernels for 0%

commit v1 on v0

v1 whole, which is shorter than its diff:
```python
import functools

import jax
import jax.numpy as jnp
from jax import lax
from jax.experimental import pallas as pl
from jax.experimental.pallas import tpu as pltpu
from jax.sharding import PartitionSpec as P

KS = 7
ROLLOUT = 8
HALF = KS // 2
EDGE = 8
epsilon = 1e-05
F32 = jnp.float32
BF16 = jnp.bfloat16
MESH = pl.DeviceIdType.MESH


def with_halo(value):
    for axis, dim, width in (("lat", 1, HALF), ("lon", 2, EDGE)):
        count, length = (lax.axis_size(axis), value.shape[dim])
        up = [(i, (i + 1) % count) for i in range(count - 1)]
        down = [(j, i) for i, j in up]
        last = lax.slice_in_dim(value, length - width, length, axis=dim)
        initial = lax.slice_in_dim(value, 0, width, axis=dim)
        before = lax.ppermute(last, axis, up)
        after = lax.ppermute(initial, axis, down)
        value = jnp.concatenate([before, value, after], axis=dim)
    return value


def merge_sum(slots, count):
    total = slots[0]
    for k in range(1, count):
        total = total + slots[k]
    return total


def merge_moments(slots, count):
    cells = slots[0][2:3]
    weighted = slots[0][2:3] * slots[0][0:1]
    for k in range(1, count):
        cells = cells + slots[k][2:3]
        weighted = weighted + slots[k][2:3] * slots[k][0:1]
    mean = weighted / jnp.maximum(cells, 1.0)
    squares = None
    for k in range(count):
        off = slots[k][0:1] - mean
        term = slots[k][1:2] + slots[k][2:3] * off * off
        squares = term if squares is None else squares + term
    return jnp.concatenate([mean, squares, cells, jnp.zeros((5, mean.shape[1]), F32)], axis=0)


def exchange_kernel(merge, sizes, x_ref, o_ref, buf0, mid, buf1, send0, recv0, send1, recv1):
    axes = ("lat", "lon")
    barrier = pltpu.get_barrier_semaphore()
    places = [lax.axis_index(a) for a in axes]
    for axis, size, me in zip(axes, sizes, places):
        for d in range(1, size):
            pl.semaphore_signal(
                barrier, inc=1, device_id={axis: lax.rem(me + d, size)}, device_id_type=MESH
            )
    pl.semaphore_wait(barrier, sum(sizes) - 2)
    stages = ((x_ref, buf0, send0, recv0, mid), (mid, buf1, send1, recv1, o_ref))
    for axis, size, me, (src, buf, send, recv, dst) in zip(axes, sizes, places, stages):
        copies = []
        for d in range(1, size):
            copy = pltpu.make_async_remote_copy(
                src_ref=src,
                dst_ref=buf.at[me],
                send_sem=send.at[d],
                recv_sem=recv.at[me],
                device_id={axis: lax.rem(me + d, size)},
                device_id_type=MESH,
            )
            copy.start()
            copies.append(copy)
        buf[me] = src[...]
        for d in range(1, size):
            other = lax.rem(me + d, size)
            pltpu.make_async_remote_copy(
                src_ref=src,
                dst_ref=buf.at[other],
                send_sem=send.at[d],
                recv_sem=recv.at[other],
                device_id={axis: other},
                device_id_type=MESH,
            ).wait_recv()
        dst[...] = merge([buf[k] for k in range(size)], size)
        for copy in copies:
            copy.wait_send()


def exchange(merge, value, number):
    sizes = (lax.axis_size("lat"), lax.axis_size("lon"))
    rows, lanes = value.shape
    return pl.pallas_call(
        functools.partial(exchange_kernel, merge, sizes),
        out_shape=jax.ShapeDtypeStruct(value.shape, F32),
        in_specs=[pl.BlockSpec(memory_space=pltpu.VMEM)],
        out_specs=pl.BlockSpec(memory_space=pltpu.VMEM),
        scratch_shapes=[
            pltpu.VMEM((sizes[0], rows, lanes), F32),
            pltpu.VMEM((rows, lanes), F32),
            pltpu.VMEM((sizes[1], rows, lanes), F32),
            pltpu.SemaphoreType.DMA((sizes[0],)),
            pltpu.SemaphoreType.DMA((sizes[0],)),
            pltpu.SemaphoreType.DMA((sizes[1],)),
            pltpu.SemaphoreType.DMA((sizes[1],)),
        ],
        compiler_params=pltpu.CompilerParams(collective_id=number, has_side_effects=True),
        name="exchange" + str(number),
    )(value)


def spread_kernel(ker_ref, taps):
    for t in range(KS * KS):
        taps[t] = jnp.broadcast_to(ker_ref[t : t + 1, :].astype(F32), (8, 128))


def conv_tile(rows_ref, taps, strip, height, flip):
    sums = [None] * height
    for j in range(KS):
        column = [taps[KS * KS - 1 - (i * KS + j) if flip else i * KS + j] for i in range(KS)]
        for r in range(height + KS - 1):
            x = rows_ref[r, pl.ds(strip * 8 + EDGE - HALF + j, 8), :]
            for i in range(KS):
                h = r - i
                if 0 <= h < height:
                    term = column[i] * x
                    sums[h] = term if sums[h] is None else sums[h] + term
    return sums


def forward_kernel(p_ref, ker_ref, o_ref, rows_ref, taps):
    batches, height, width, _ = o_ref.shape
    spread_kernel(ker_ref, taps)

    def batch(m, carry):
        for r in range(height + KS - 1):
            rows_ref[r] = p_ref[m, r].astype(F32)
        for strip in range(width // 8):
            sums = conv_tile(rows_ref, taps, strip, height, False)
            for h in range(height):
                o_ref[m, h, pl.ds(strip * 8, 8), :] = sums[h]
        return carry

    lax.fori_loop(0, batches, batch, 0)


def depthwise(padded, kernel, shape):
    batches, height, width, channels = shape
    tall, wide = height + KS - 1, width + 2 * EDGE
    return pl.pallas_call(
        forward_kernel,
        grid=(pl.cdiv(channels, 128),),
        in_specs=[
            pl.BlockSpec((batches, tall, wide, 128), lambda c: (0, 0, 0, c)),
            pl.BlockSpec((KS * KS, 128), lambda c: (0, c)),
        ],
        out_specs=pl.BlockSpec((batches, height, width, 128), lambda c: (0, 0, 0, c)),
        out_shape=jax.ShapeDtypeStruct(shape, F32),
        scratch_shapes=[pltpu.VMEM((tall, wide, 128), F32), pltpu.VMEM((KS * KS, 8, 128), F32)],
        name="depthwise",
    )(padded, kernel)


def backward_kernel(
    p_ref, d_ref, ker_ref, g_ref, share_ref, o_ref, k_ref, rows_ref, grads_ref, taps, sums_ref
):
    batches, height, width, _ = o_ref.shape
    spread_kernel(ker_ref, taps)
    sums_ref[...] = jnp.zeros_like(sums_ref)

    def batch(m, carry):
        for r in range(height + KS - 1):
            rows_ref[r] = p_ref[m, r].astype(F32)
            grads_ref[r] = d_ref[m, r].astype(F32)
        share = share_ref[m]
        for strip in range(width // 8):
            sums = conv_tile(grads_ref, taps, strip, height, True)
            for h in range(height):
                g = g_ref[m, h, pl.ds(strip * 8, 8), :].astype(F32) * share
                o_ref[m, h, pl.ds(strip * 8, 8), :] = (g + sums[h]).astype(BF16)
            own = [grads_ref[h + HALF, pl.ds(strip * 8 + EDGE, 8), :] for h in range(height)]
            for j in range(KS):
                parts = [sums_ref[i * KS + j] for i in range(KS)]
                for r in range(height + KS - 1):
                    x = rows_ref[r, pl.ds(strip * 8 + EDGE - HALF + j, 8), :]
                    for i in range(KS):
                        h = r - i
                        if 0 <= h < height:
                            parts[i] = parts[i] + own[h] * x
                for i in range(KS):
                    sums_ref[i * KS + j] = parts[i]
        return carry

    lax.fori_loop(0, batches, batch, 0)
    for t in range(KS * KS):
        k_ref[t : t + 1, :] = jnp.sum(sums_ref[t], axis=0, keepdims=True)


def depthwise_back(padded, d_padded, kernel, cotangent, shares):
    batches, height, width, channels = cotangent.shape
    tall, wide = height + KS - 1, width + 2 * EDGE
    tile = pl.BlockSpec((batches, tall, wide, 128), lambda c: (0, 0, 0, c))
    own = pl.BlockSpec((batches, height, width, 128), lambda c: (0, 0, 0, c))
    taps = pl.BlockSpec((KS * KS, 128), lambda c: (0, c))
    return pl.pallas_call(
        backward_kernel,
        grid=(pl.cdiv(channels, 128),),
        in_specs=[tile, tile, taps, own, pl.BlockSpec(memory_space=pltpu.SMEM)],
        out_specs=[own, taps],
        out_shape=[
            jax.ShapeDtypeStruct(cotangent.shape, BF16),
            jax.ShapeDtypeStruct((KS * KS, channels), F32),
        ],
        scratch_shapes=[
            pltpu.VMEM((tall, wide, 128), F32),
            pltpu.VMEM((tall, wide, 128), F32),
            pltpu.VMEM((KS * KS, 8, 128), F32),
            pltpu.VMEM((KS * KS, 8, 128), F32),
        ],
        name="depthwise_back",
    )(padded, d_padded, kernel, cotangent, shares)


def smooth_gate(values):
    return jax.nn.gelu(values, approximate=True)


def body(
    inputs,
    conv_kernel,
    norm_gain,
    norm_shift,
    w_in,
    b_in,
    w_out,
    b_out,
    ocean_mask,
    lengths,
    cotangent,
):
    batches, tile_rows, tile_cols, channels = inputs.shape
    padded = with_halo(inputs)
    taps = conv_kernel.reshape(KS * KS, channels)
    convolved = depthwise(padded, taps, inputs.shape)
    ocean_cells = ocean_mask.astype(F32)[None, :, :, None]
    local_count = jnp.sum(ocean_mask).astype(F32) * batches
    local_mean = jnp.sum(convolved * ocean_cells, axis=(0, 1, 2)) / jnp.maximum(local_count, 1.0)
    off = convolved - local_mean
    local_squares = jnp.sum(off * off * ocean_cells, axis=(0, 1, 2))
    moments = jnp.zeros((8, channels), F32)
    moments = moments.at[0].set(local_mean).at[1].set(local_squares).at[2].set(local_count)
    moments = exchange(merge_moments, moments, 0)
    mean_value, cell_count = moments[0], moments[2, 0]
    inv_std = lax.rsqrt(moments[1] / cell_count + epsilon)
    standard = (convolved - mean_value) * inv_std
    gain_vec = norm_gain.astype(F32)
    normed = (standard * gain_vec + norm_shift.astype(F32)).astype(BF16).reshape(-1, channels)
    pre_gate = jnp.dot(normed, w_in, preferred_element_type=F32) + b_in.astype(F32)
    activated, gate_back = jax.vjp(smooth_gate, pre_gate)
    act_low = activated.astype(BF16)
    branch = jnp.dot(act_low, w_out, preferred_element_type=F32) + b_out.astype(F32)
    output = (inputs.astype(F32) + ocean_cells * branch.reshape(inputs.shape)).astype(BF16)
    kept_steps = lengths.astype(F32) / ROLLOUT
    d_output = cotangent.astype(F32) * kept_steps[:, None, None, None]
    d_branch = (d_output * ocean_cells).reshape(-1, channels)
    branch_low = d_branch.astype(BF16)
    local_b_out = jnp.sum(d_branch, axis=0)
    local_w_out = lax.dot_general(
        act_low, branch_low, (((0,), (0,)), ((), ())), preferred_element_type=F32
    ).astype(BF16)
    d_act = lax.dot_general(branch_low, w_out, (((1,), (1,)), ((), ())), preferred_element_type=F32)
    d_pre = gate_back(d_act)[0]
    pre_low = d_pre.astype(BF16)
    local_b_in = jnp.sum(d_pre, axis=0)
    local_w_in = lax.dot_general(
        normed, pre_low, (((0,), (0,)), ((), ())), preferred_element_type=F32
    ).astype(BF16)
    d_normed = lax.dot_general(
        pre_low, w_in, (((1,), (1,)), ((), ())), preferred_element_type=F32
    ).reshape(inputs.shape)
    sums = jnp.zeros((8, channels), F32)
    sums = sums.at[0].set(jnp.sum(d_normed, axis=(0, 1, 2)))
    sums = sums.at[1].set(jnp.sum(d_normed * standard, axis=(0, 1, 2)))
    sums = sums.at[2].set(local_b_out)
    spread = pl.cdiv(b_in.shape[0], channels)
    sums = sums.at[3 : 3 + spread].set(
        jnp.pad(local_b_in, (0, spread * channels - b_in.shape[0])).reshape(spread, channels)
    )
    sums = exchange(merge_sum, sums, 1)
    d_shift, d_gain, d_b_out = sums[0], sums[1], sums[2]
    d_b_in = sums[3 : 3 + spread].reshape(-1)[: b_in.shape[0]]
    d_conv = (
        gain_vec * inv_std * (d_normed - ocean_cells * (d_shift + standard * d_gain) / cell_count)
    )
    d_padded = with_halo(d_conv.astype(BF16))
    d_inputs, local_kernel = depthwise_back(padded, d_padded, taps, cotangent, kept_steps)
    d_w_in, d_w_out = lax.psum((local_w_in, local_w_out), ("lat", "lon"))
    d_kernel = lax.psum(local_kernel, ("lat", "lon"))
    return (
        output,
        d_inputs,
        d_kernel.reshape(conv_kernel.shape),
        d_gain,
        d_shift,
        d_w_in.astype(F32),
        d_b_in,
        d_w_out.astype(F32),
        d_b_out,
    )


def solution(mesh):
    tile = P(None, "lat", "lon", None)
    in_specs = (tile, P(), P(), P(), P(), P(), P(), P(), P("lat", "lon"), P(), tile)
    out_specs = (tile, tile, P(), P(), P(), P(), P(), P(), P())
    return jax.shard_map(body, mesh=mesh, in_specs=in_specs, out_specs=out_specs, check_vma=False)
```

time: 811 us -> 528 us (0.65)
  other arithmetic: 316 us -> 43.3 us
  blocking collectives: 128 us -> 0 us
  Pallas kernels: 0 us -> 82.4 us
  waiting for transfers between devices: 213 us -> 266 us
    reduce_sum x6 -> x3, other arithmetic: 187 us -> 7.1 us  [the longest x1 3.88 us: body(): sums = sums.at[1].set(jnp.sum(d_normed * standard, axis=(0, 1, 2)))]
    psum x3 -> x0, blocking collectives: 128 us -> none  [the longest x1 46.7 us: body(): lax.psum((jnp.sum(masked, axis=(0, 1, 2)), local_count), ('lat', 'lon'))]
    convert_element_type x10 -> x8, other arithmetic: 122 us -> 23.1 us  [the longest x1 7.27 us: body(): d_w_in.astype(F32)]
    pallas_call x0 -> x4, Pallas kernels: none -> 82.4 us  [the longest x2 40.5 us: exchange(): pl.pallas_call(functools.partial(exchange_kernel, merge, sizes), out_shap...]
    psum x1 -> x2, waiting for transfers between devices: 184 us -> 222 us  [the longest x1 118 us: body(): d_kernel = lax.psum(local_kernel, ('lat', 'lon'))]
    ppermute x4, waiting for transfers between devices: 14.2 us -> 35 us  [with_halo(): before = lax.ppermute(last, axis, up)]
    unnamed x211 -> x47, local copies, waits for them, and re-layouts: 17.7 us -> 5.52 us
  transfers between devices with their start and end apart: 9 -> 10, of which waited for: 5 -> 9; matrix products, arithmetic and copies ran while one was open for 17% -> 9% of each run, Pallas kernels for 0% -> 8%
where the time goes in v1:
time: 528 us; the launch traced here: 526 us
  waiting for transfers between devices  266 us (50%)
  Pallas kernels  82.4 us (16%)
  matrix products  75.2 us (14%)
  other arithmetic  43.3 us (8%)
  local copies, waits for them, and re-layouts  25.4 us (5%)
  starting transfers between devices  18.4 us (3%)
  between operations  15.1 us (3%)
    psum x1, waiting for transfers between devices, body(): d_kernel = lax.psum(local_kernel, ('lat', 'lon'))  118 us
    psum x1, waiting for transfers between devices, body(): d_w_in, d_w_out = lax.psum((local_w_in, local_w_out), ('lat', 'lon'))  104 us
    pallas_call x2, Pallas kernels, exchange(): pl.pallas_call(functools.partial(exchange_kernel, merge, sizes), out_shap...  40.5 us
    ppermute x4, waiting for transfers between devices, with_halo(): before = lax.ppermute(last, axis, up)  35 us
    pallas_call x1, Pallas kernels, depthwise_back(): pl.pallas_call(backward_kernel, grid=(pl.cdiv(channels, 128),), in_specs=...  27.6 us
    dot_general x1, matrix products, body(): lax.dot_general(branch_low, w_out, (((1,), (1,)), ((), ())), preferred_el...  17.4 us
    pallas_call x1, Pallas kernels, depthwise(): pl.pallas_call(forward_kernel, grid=(pl.cdiv(channels, 128),), in_specs=[...  14.4 us
    dot_general x1, matrix products, body(): jnp.dot(normed, w_in, preferred_element_type=F32) + b_in.astype(F32)  13.3 us
  transfers between devices with their start and end apart: 10, of which 9 were waited for; matrix products, arithmetic and copies ran while one was open for 9% of the time, Pallas kernels for 8%

profile of v1, /device:TPU:0, one launch (start us, length us, event | category | flops | bytes accessed | tf_op | source)
XLA Modules:
  0.0 526.3 jit_solution(15837189588823159103)
XLA Ops:
  8.8 5.0 collective-permute-start
  15.3 13.1 %collective-permute-done = bf16[4,3,32,800]{3,2,1,0:T(8,128)(2,1)S(1)} collective-permute-done((bf16[4,3,32,800]{3,2,1,0:T(8,128)(2,1)S(1)}, bf16[4,3,32,800]{3,2,1,0:T(8,128)(2,1)S(1)}, u32[]{:S(2)}, u32[]{:S(2)}) %collective-permute-start) | collective-permute-done | bytes 614432 | tf_op jit(solution)/shard_map/ppermute | solution.py:27
  28.9 3.9 collective-permute-done.1
  32.9 1.7 copy-done.2
  43.3 4.5 pad_maximum_fusion.p_ref
  47.8 14.4 %depthwise.1 = f32[4,8,32,800]{3,2,1,0:T(8,128)} custom-call(bf16[4,14,48,800]{3,2,1,0:T(8,128)(2,1)} %pad_maximum_fusion.p_ref, bf16[49,800]{1,0:T(8,128)(2,1)} %reshape.239.ker_ref), custom_call_target="tpu_custom_call" | custom-call | tf_op jit(solution)/shard_map/depthwise/pallas_call | solution.py:155
  62.2 2.6 multiply_reduce_fusion.2
  65.3 3.9 fusion.6
  70.2 27.3 %exchange0.1 = f32[8,800]{1,0:T(8,128)} custom-call(f32[8,800]{1,0:T(8,128)} %copy-done.7), custom_call_target="tpu_custom_call" | custom-call | tf_op jit(solution)/shard_map/exchange0/pallas_call | solution.py:98
  100.2 2.6 add_convert_fusion.1
  102.9 13.3 %fusion.18 = f32[1024,3200]{1,0:T(8,128)} fusion(bf16[1024,800]{1,0:T(8,128)(2,1)S(1)} %bitcast.20, bf16[800,3200]{1,0:T(8,128)(2,1)} %param.29), kind=kOutput, calls=%fused_computation.47 | convolution fusion | flops 5242880000 | bytes 19865600 | tf_op jit(solution)/shard_map/dot_general | solution.py:263
  116.3 12.0 %convolution_convert_fusion = bf16[3200,800]{0,1:T(8,128)(2,1)} fusion(bf16[1024,800]{1,0:T(8,128)(2,1)S(1)} %bitcast.18, f32[1024,3200]{1,0:T(8,128)} %fusion.18, f32[3200]{0:T(1024)S(1)} %copy-done.10), kind=kOutput, calls=%fused_computation.9 | convolution fusion | flops 5278208000 | bytes 19878400 | tf_op jit(solution)/shard_map/dot_general | solution.py:273
  128.3 17.4 %fusion.11 = (f32[3200]{0:T(1024)S(1)}, bf16[1024,3200]{1,0:T(8,128)(2,1)}) fusion(f32[1024,3200]{1,0:T(8,128)} %fusion.18, f32[3200]{0:T(1024)S(1)} %copy-done.10, bf16[1024,800]{1,0:T(8,128)(2,1)S(1)} %bitcast.19, bf16[3200,800]{0,1:T(8,128)(2,1)S(1)} %bitcast.23), kind=kOutput, calls=%fused_computation.41 | convolution fusion | flops 5314966528 | bytes 26444800 | tf_op jit(solution)/shard_map/dot_general | solution.py:276
  145.6 10.3 %convolution_add_fusion = f32[1024,800]{0,1:T(8,128)} fusion(bf16[3200,800]{0,1:T(8,128)(2,1)S(1)} %bitcast.23, f32[800]{0:T(1024)S(1)} %copy-done.15, f32[1024,3200]{1,0:T(8,128)} %fusion.18, f32[3200]{0:T(1024)S(1)} %copy-done.10), kind=kOutput, calls=%fused_computation.26 | convolution fusion | flops 5276467200 | bytes 21520000 | tf_op jit(solution)/shard_map/dot_general | solution.py:266
  155.9 4.9 copy.20
  161.0 11.5 %convolution_convert_fusion.1 = bf16[800,3200]{1,0:T(8,128)(2,1)} fusion(bf16[1024,800]{1,0:T(8,128)(2,1)} %bitcast.21, bf16[1024,3200]{1,0:T(8,128)(2,1)} %get-tuple-element.107), kind=kOutput, calls=%fused_computation.10 | convolution fusion | flops 5245440000 | bytes 13312000 | tf_op jit(solution)/shard_map/dot_general | solution.py:280
  172.5 10.7 %fusion.17 = (f32[800]{0:T(1024)S(1)}, f32[1024,800]{0,1:T(8,128)}) fusion(bf16[800,3200]{1,0:T(8,128)(2,1)} %param.29, bf16[1024,3200]{1,0:T(8,128)(2,1)} %get-tuple-element.107), kind=kOutput, calls=%fused_computation.46 | convolution fusion | flops 5243698176 | bytes 14953600 | tf_op jit(solution)/shard_map/dot_general | solution.py:283
  183.2 4.9 copy.21
  188.2 3.9 multiply_reduce_fusion
  193.4 13.1 %exchange1.1 = f32[8,800]{1,0:T(8,128)} custom-call(f32[8,800]{1,0:T(8,128)} %copy-done.6), custom_call_target="tpu_custom_call" | custom-call | tf_op jit(solution)/shard_map/exchange1/pallas_call | solution.py:98
  208.0 6.7 %multiply_convert_fusion.1 = (bf16[4,8,32,800]{3,2,1,0:T(8,128)(2,1)S(1)}, bf16[4,8,32,800]{3,2,1,0:T(8,128)(2,1)}) fusion(f32[4,8,32,800]{3,2,1,0:T(8,128)} %depthwise.1, f32[]{:T(128)} %bitcast, f32[800]{0:T(1024)S(1)} %get-tuple-element.128, f32[800]{0:T(1024)S(1)} %get-tuple-element.129, f32[800]{0:T(1024)S(1)} %convert_multiply_fusion, ...), kind=kLoop, calls=%fused_computation.13 | loop fusion | flops 10649600 | bytes 14762628 | tf_op jit(solution)/shard_map/convert_element_type | solution.py:300
  214.8 4.6 collective-permute-start.4
  220.8 21.3 %collective-permute-done.4 = bf16[4,3,32,800]{3,2,1,0:T(8,128)(2,1)S(1)} collective-permute-done((bf16[4,3,32,800]{3,2,1,0:T(8,128)(2,1)S(1)}, bf16[4,3,32,800]{3,2,1,0:T(8,128)(2,1)S(1)}, u32[]{:S(2)}, u32[]{:S(2)}) %collective-permute-start.4) | collective-permute-done | bytes 614432 | tf_op jit(solution)/shard_map/ppermute | solution.py:27
  242.1 2.5 collective-permute-done.5
  244.7 2.1 collective-permute-start.6
  248.6 3.3 collective-permute-done.7
  251.9 2.4 pad_maximum_fusion.1.d_ref
  254.3 27.6 %depthwise_back.1 = (bf16[4,8,32,800]{3,2,1,0:T(8,128)(2,1)}, f32[49,800]{1,0:T(8,128)}) custom-call(bf16[4,14,48,800]{3,2,1,0:T(8,128)(2,1)} %pad_maximum_fusion.p_ref, bf16[4,14,48,800]{3,2,1,0:T(8,128)(2,1)} %pad_maximum_fusion.1.d_ref, bf16[49,800]{1,0:T(8,128)(2,1)} %reshape.239.ker_ref, bf16[4,8,32,800]{3,2,1,0:T(8,128)(2,1)} %g_ref.1, f32[4]{0:T(128)} %copy-done.19), custom_call_target="tpu_custom_call" | custom-call | tf_op jit(solution)/shard_map/depthwise_back/pallas_call | solution.py:210
  284.3 103.5 %all-reduce.8.cloned.1.call-done = (bf16[800,3200]{1,0:T(8,128)(2,1)}, bf16[3200,800]{0,1:T(8,128)(2,1)}) async-done(((bf16[800,3200]{1,0:T(8,128)(2,1)}, bf16[3200,800]{0,1:T(8,128)(2,1)}), (bf16[800,3200]{1,0:T(8,128)(2,1)}, bf16[3200,800]{0,1:T(8,128)(2,1)})) %all-reduce.8.cloned.1.call-update) | async-done | bytes 10240016 | tf_op jit(solution)/shard_map/psum | solution.py:302
  387.8 7.3 %convert_element_type.77 = f32[800,3200]{1,0:T(8,128)} convert(bf16[800,3200]{1,0:T(8,128)(2,1)} %get-tuple-element.104) | non-fusion elementwise | flops 2560000 | bytes 15360000 | tf_op jit(solution)/shard_map/convert_element_type | solution.py:310
  395.1 4.7 convert_element_type.79
  399.7 118.1 %all-reduce.6.cloned.1.call-done = f32[7,7,800]{2,1,0:T(8,128)} async-done(((f32[7,7,800]{2,1,0:T(8,128)}), f32[7,7,800]{2,1,0:T(8,128)}) %all-reduce.6.cloned.1.call-update) | async-done | bytes 156816 | tf_op jit(solution)/shard_map/psum | solution.py:303
  (93 shorter events, 26.1 us)
Async XLA Ops:
  7.2 21.3 %copy-start.1 = (bf16[4,8,32,800]{3,2,1,0:T(8,128)(2,1)S(1)}, bf16[4,8,32,800]{3,2,1,0:T(8,128)(2,1)}, u32[]{:S(2)}) copy-start(bf16[4,8,32,800]{3,2,1,0:T(8,128)(2,1)} %param.25) | copy-start | bytes 4915204
  7.2 380.6 %all-reduce.8.cloned.1.call-start = ((), (), s32[]{:S(2)}) async-start(), calls=%async_computation.1 | async-start | bytes 20480000 | tf_op jit(solution)/shard_map/psum | solution.py:302
  8.8 19.6 %collective-permute-start = (bf16[4,3,32,800]{3,2,1,0:T(8,128)(2,1)S(1)}, bf16[4,3,32,800]{3,2,1,0:T(8,128)(2,1)S(1)}, u32[]{:S(2)}, u32[]{:S(2)}) collective-permute-start(bf16[4,3,32,800]{3,2,1,0:T(8,128)(2,1)S(1)} %get-tuple-element.116), channel_id=1, source_target_pairs={{0,8},{8,16},{16,24},{1,9},{9,17},{17,25},{2,10},{10,18},{18,26},{... | collective-permute-start | bytes 1843208 | tf_op jit(solution)/shard_map/ppermute | solution.py:27
  13.8 24.7 %copy-start.17 = (bf16[800]{0:T(1024)(128)(2,1)S(1)}, bf16[800]{0:T(1024)(128)(2,1)}, u32[]{:S(2)}) copy-start(bf16[800]{0:T(1024)(128)(2,1)} %param.28) | copy-start | bytes 4804
  13.8 24.7 %copy-start.18 = (bf16[800]{0:T(1024)(128)(2,1)S(1)}, bf16[800]{0:T(1024)(128)(2,1)}, u32[]{:S(2)}) copy-start(bf16[800]{0:T(1024)(128)(2,1)} %param.32) | copy-start | bytes 4804
  13.8 25.3 %copy-start.13 = (bf16[800]{0:T(1024)(128)(2,1)S(1)}, bf16[800]{0:T(1024)(128)(2,1)}, u32[]{:S(2)}) copy-start(bf16[800]{0:T(1024)(128)(2,1)} %param.27) | copy-start | bytes 4804
  13.8 25.3 %copy-start.16 = (s32[8,32]{1,0:T(8,128)S(1)}, s32[8,32]{1,0:T(8,128)}, u32[]{:S(2)}) copy-start(s32[8,32]{1,0:T(8,128)} %param.33) | copy-start | bytes 3076
  13.8 27.9 %copy-start.9 = (bf16[7,7,800]{2,1,0:T(8,128)(2,1)S(1)}, bf16[7,7,800]{2,1,0:T(8,128)(2,1)}, u32[]{:S(2)}) copy-start(bf16[7,7,800]{2,1,0:T(8,128)(2,1)} %param.26) | copy-start | bytes 235204
  13.8 18.9 %collective-permute-start.1 = (bf16[4,3,32,800]{3,2,1,0:T(8,128)(2,1)S(1)}, bf16[4,3,32,800]{3,2,1,0:T(8,128)(2,1)S(1)}, u32[]{:S(2)}, u32[]{:S(2)}) collective-permute-start(bf16[4,3,32,800]{3,2,1,0:T(8,128)(2,1)S(1)} %get-tuple-element.115), channel_id=1, source_target_pairs={{8,0},{16,8},{24,16},{9,1},{17,9},{25,17},{10,2},{18,10},{26,18},{... | collective-permute-start | bytes 1843208 | tf_op jit(solution)/shard_map/ppermute | solution.py:28
  32.9 1.7 copy-start.2
  35.8 7.2 %collective-permute-start.2 = (bf16[4,14,8,800]{3,2,1,0:T(8,128)(2,1)}, bf16[4,14,8,800]{3,2,1,0:T(8,128)(2,1)S(1)}, u32[]{:S(2)}, u32[]{:S(2)}) collective-permute-start(bf16[4,14,8,800]{3,2,1,0:T(8,128)(2,1)} %get-tuple-element.110), channel_id=1, source_target_pairs={{0,1},{1,2},{2,3},{3,4},{4,5},{5,6},{6,7},{8,9},{9,10},{10,11},{11... | collective-permute-start | bytes 2150408 | tf_op jit(solution)/shard_map/ppermute | solution.py:27
  37.2 6.1 %collective-permute-start.3 = (bf16[4,14,8,800]{3,2,1,0:T(8,128)(2,1)}, bf16[4,14,8,800]{3,2,1,0:T(8,128)(2,1)S(1)}, u32[]{:S(2)}, u32[]{:S(2)}) collective-permute-start(bf16[4,14,8,800]{3,2,1,0:T(8,128)(2,1)} %get-tuple-element.111), channel_id=1, source_target_pairs={{1,0},{2,1},{3,2},{4,3},{5,4},{6,5},{7,6},{9,8},{10,9},{11,10},{12... | collective-permute-start | bytes 2150408 | tf_op jit(solution)/shard_map/ppermute | solution.py:28
  43.1 21.7 %copy-start.19 = (f32[4]{0:T(128)}, f32[4]{0:T(128)S(1)}, u32[]{:S(2)}) copy-start(f32[4]{0:T(128)S(1)} %convert_multiply_fusion.1.share_ref) | copy-start | bytes 52
  62.2 3.1 copy-start
  69.6 0.6 copy-start.7
  102.9 13.4 %copy-start.5 = (bf16[4,8,32,800]{3,2,1,0:T(8,128)(2,1)}, bf16[4,8,32,800]{3,2,1,0:T(8,128)(2,1)S(1)}, u32[]{:S(2)}) copy-start(bf16[4,8,32,800]{3,2,1,0:T(8,128)(2,1)S(1)} %add_convert_fusion.1) | copy-start | bytes 4915204
  102.9 13.3 %copy-start.4 = (bf16[4,8,32,800]{3,2,1,0:T(8,128)(2,1)S(1)}, bf16[4,8,32,800]{3,2,1,0:T(8,128)(2,1)}, u32[]{:S(2)}) copy-start(bf16[4,8,32,800]{3,2,1,0:T(8,128)(2,1)} %get-tuple-element.112) | copy-start | bytes 4915204
  102.9 13.3 %copy-start.10 = (f32[3200]{0:T(1024)S(1)}, f32[3200]{0:T(1024)}, u32[]{:S(2)}) copy-start(f32[3200]{0:T(1024)} %convert_element_type.66) | copy-start | bytes 38404
  102.9 25.3 %slice-start = ((s8[5120000]{0:T(1024)(128)(4,1)}), s8[4194304]{0:T(1024)(128)(4,1)S(1)}, s32[]{:S(2)}) async-start(s8[5120000]{0:T(1024)(128)(4,1)} %bitcast.22), calls=%async_computation.2 | async-start | bytes 8388608
  116.2 12.0 %slice-start.1 = ((s8[5120000]{0:T(1024)(128)(4,1)}), s8[925696]{0:T(1024)(128)(4,1)S(1)}, s32[]{:S(2)}) async-start(s8[5120000]{0:T(1024)(128)(4,1)} %bitcast.22), calls=%async_computation.3 | async-start | bytes 1851392
  128.3 17.4 %copy-start.15 = (f32[800]{0:T(1024)S(1)}, f32[800]{0:T(1024)}, u32[]{:S(2)}) copy-start(f32[800]{0:T(1024)} %convert_element_type.68) | copy-start | bytes 9604
  172.5 345.4 %all-reduce.6.cloned.1.call-start = ((), (), s32[]{:S(2)}) async-start(), calls=%async_computation | async-start | bytes 401408 | tf_op jit(solution)/shard_map/psum | solution.py:303
  188.2 19.8 %copy-start.14 = (bf16[800]{0:T(1024)(128)(2,1)S(1)}, bf16[800]{0:T(1024)(128)(2,1)}, u32[]{:S(2)}) copy-start(bf16[800]{0:T(1024)(128)(2,1)} %param.27) | copy-start | bytes 4804
  192.7 0.6 copy-start.6
  208.0 6.7 %copy-start.11 = (f32[800]{0:T(1024)}, f32[800]{0:T(1024)S(1)}, u32[]{:S(2)}) copy-start(f32[800]{0:T(1024)S(1)} %get-tuple-element.128) | copy-start | bytes 9604
  208.0 6.7 %copy-start.12 = (f32[800]{0:T(1024)}, f32[800]{0:T(1024)S(1)}, u32[]{:S(2)}) copy-start(f32[800]{0:T(1024)S(1)} %get-tuple-element.129) | copy-start | bytes 9604
  214.8 27.2 %collective-permute-start.4 = (bf16[4,3,32,800]{3,2,1,0:T(8,128)(2,1)S(1)}, bf16[4,3,32,800]{3,2,1,0:T(8,128)(2,1)S(1)}, u32[]{:S(2)}, u32[]{:S(2)}) collective-permute-start(bf16[4,3,32,800]{3,2,1,0:T(8,128)(2,1)S(1)} %get-tuple-element.113), channel_id=1, source_target_pairs={{0,8},{8,16},{16,24},{1,9},{9,17},{17,25},{2,10},{10,18},{18,26},{... | collective-permute-start | bytes 1843208 | tf_op jit(solution)/shard_map/ppermute | solution.py:27
  219.5 25.1 %collective-permute-start.5 = (bf16[4,3,32,800]{3,2,1,0:T(8,128)(2,1)S(1)}, bf16[4,3,32,800]{3,2,1,0:T(8,128)(2,1)S(1)}, u32[]{:S(2)}, u32[]{:S(2)}) collective-permute-start(bf16[4,3,32,800]{3,2,1,0:T(8,128)(2,1)S(1)} %get-tuple-element.114), channel_id=1, source_target_pairs={{8,0},{16,8},{24,16},{9,1},{17,9},{25,17},{10,2},{18,10},{26,18},{... | collective-permute-start | bytes 1843208 | tf_op jit(solution)/shard_map/ppermute | solution.py:28
  244.7 3.9 collective-permute-start.6
  246.7 5.1 collective-permute-start.7
  254.3 29.3 %copy-start.8 = (f32[8,800]{1,0:T(8,128)S(1)}, f32[8,800]{1,0:T(8,128)}, u32[]{:S(2)}) copy-start(f32[8,800]{1,0:T(8,128)} %exchange1.1) | copy-start | bytes 76804
  387.8 7.3 %copy-start.3 = (bf16[3200,800]{0,1:T(8,128)(2,1)S(1)}, bf16[3200,800]{0,1:T(8,128)(2,1)}, u32[]{:S(2)}) copy-start(bf16[3200,800]{0,1:T(8,128)(2,1)} %get-tuple-element.105) | copy-start | bytes 15360004
Sparse Core Ops, SparseCore 0:
  172.6 215.1 all-reduce.7
  393.3 124.4 all-reduce.5

commit v2 on v1

--- a/solution.py
+++ b/solution.py
@@ -11,6 +11,8 @@
 ROLLOUT = 8
 HALF = KS // 2
 EDGE = 8
+UNITS = 16
+LAG = 2
 epsilon = 1e-05
 F32 = jnp.float32
 BF16 = jnp.bfloat16
@@ -112,6 +114,235 @@
         compiler_params=pltpu.CompilerParams(collective_id=number, has_side_effects=True),
         name="exchange" + str(number),
     )(value)
+
+
+class Ring:
+    STEPS = 9
+
+    def __init__(self, side, lats, grads, result, part, work, land0, land, gat, send, recv, local):
+        self.grads, self.result, self.local = grads, result, local
+        self.side, self.lats = side, lats
+        self.part, self.work, self.land0, self.land, self.gat = part, work, land0, land, gat
+        self.send, self.recv = send, recv
+        self.units = part.shape[2]
+        lon, lat = lax.axis_index("lon"), lax.axis_index("lat")
+        core = lax.rem(lon, 2)
+        pair = lon // 2
+        a, b = pair // side, lax.rem(pair, side)
+        first = a * (1 - core) + b * core
+        second = b * (1 - core) + a * core
+        wide = 2 * side * (1 - core) + 2 * core
+        narrow = 2 * (1 - core) + 2 * side * core
+        self.core, self.lon = core, lon
+        self.axes = (
+            (side, first, lambda q: {"lon": lon + (q - first) * wide}),
+            (side, second, lambda q: {"lon": lon + (q - second) * narrow}),
+            (lats, lat, lambda q: {"lat": q}),
+        )
+        sub0 = self.units // side
+        sub1 = sub0 // side
+        sub2 = sub1 // lats
+        start0 = first * sub0
+        start1 = start0 + second * sub1
+        start2 = start1 + lat * sub2
+        self.ranges = ((0, start0, sub0), (start0, start1, sub1), (start1, start2, sub2))
+
+    def barrier(self):
+        bar = pltpu.get_barrier_semaphore()
+        pl.semaphore_signal(
+            bar, inc=1, device_id={"lon": self.lon + 1 - 2 * self.core}, device_id_type=MESH
+        )
+        count = 1
+        for size, place, where in self.axes:
+            for d in range(1, size):
+                pl.semaphore_signal(bar, inc=1, device_id=where(lax.rem(place + d, size)), device_id_type=MESH)
+                count += 1
+        pl.semaphore_wait(bar, count)
+
+    def load(self, half, c):
+        return pltpu.make_async_copy(
+            self.grads.at[half, c], self.part.at[half, c], self.local.at[0, half, c]
+        )
+
+    def save(self, half, c):
+        return pltpu.make_async_copy(
+            self.gat.at[half, c], self.result.at[half, c], self.local.at[1, half, c]
+        )
+
+    def cores(self, c, out):
+        other = 1 - self.core
+        src, dst, stage = (
+            (self.gat.at[self.core, c], self.gat.at[self.core, c], 7)
+            if out
+            else (self.part.at[other, c], self.land0.at[c], 0)
+        )
+        return pltpu.make_async_remote_copy(
+            src_ref=src, dst_ref=dst, send_sem=self.send.at[c, stage, 0], recv_sem=self.recv.at[c, stage, 0],
+            device_id={"lon": self.lon + 1 - 2 * self.core}, device_id_type=MESH,
+        )
+
+    def scatter(self, c, k):
+        size, place, where = self.axes[k]
+        base, start, sub = self.ranges[k]
+        out = []
+        for d in range(1, size):
+            q = lax.rem(place + d, size)
+            out.append(pltpu.make_async_remote_copy(
+                src_ref=self.work.at[c, pl.ds(base + q * sub, sub)],
+                dst_ref=self.land[k].at[c, d - 1],
+                send_sem=self.send.at[c, 1 + k, d - 1], recv_sem=self.recv.at[c, 1 + k, d - 1],
+                device_id=where(q), device_id_type=MESH,
+            ))
+        return out
+
+    def gather(self, c, k):
+        size, place, where = self.axes[k]
+        base, start, sub = self.ranges[k]
+        out = []
+        for d in range(1, size):
+            q = lax.rem(place + d, size)
+            out.append(pltpu.make_async_remote_copy(
+                src_ref=self.gat.at[self.core, c, pl.ds(start, sub)],
+                dst_ref=self.gat.at[self.core, c, pl.ds(start, sub)],
+                send_sem=self.send.at[c, 4 + k, d - 1], recv_sem=self.recv.at[c, 4 + k, d - 1],
+                device_id=where(q), device_id_type=MESH,
+            ))
+        return out
+
+    def add(self, c, k):
+        base, start, sub = self.ranges[k]
+        total = self.work[c, pl.ds(start, sub)].astype(F32)
+        for d in range(self.axes[k][0] - 1):
+            total = total + self.land[k][c, d].astype(F32)
+        return total.astype(BF16)
+
+    def step(self, s, c):
+        if s == 0:
+            for half in range(2):
+                self.load(half, c).wait()
+            self.cores(c, False).start()
+        elif s == 1:
+            self.cores(c, False).wait()
+            self.work[c] = (self.part[self.core, c].astype(F32) + self.land0[c].astype(F32)).astype(BF16)
+            for x in self.scatter(c, 0): x.start()
+        elif s in (2, 3, 4):
+            k = s - 2
+            for x in self.scatter(c, k): x.wait()
+            base, start, sub = self.ranges[k]
+            if k < 2:
+                self.work[c, pl.ds(start, sub)] = self.add(c, k)
+                for x in self.scatter(c, k + 1): x.start()
+            else:
+                self.gat[self.core, c, pl.ds(start, sub)] = self.add(c, k)
+                for x in self.gather(c, 2): x.start()
+        elif s in (5, 6, 7):
+            k = 7 - s
+            for x in self.gather(c, k): x.wait()
+            if k:
+                for x in self.gather(c, k - 1): x.start()
+            else:
+                self.cores(c, True).start()
+        else:
+            self.cores(c, True).wait()
+            for half in range(2):
+                self.save(half, c).start()
+
+
+def reduce_kernel(
+    side, lats, grads, result, part, gat, work, land0, land1, land2, land3, send, recv, local
+):
+    ring = Ring(
+        side, lats, grads, result, part, work, land0, (land1, land2, land3), gat, send, recv, local
+    )
+    chunks = part.shape[1]
+
+    def fetch(c, carry):
+        for half in range(2):
+            ring.load(half, c).start()
+        return carry
+
+    lax.fori_loop(0, chunks, fetch, 0)
+    ring.barrier()
+
+    def tick(t, carry):
+        for s in reversed(range(Ring.STEPS)):
+            c = t - LAG * s
+
+            @pl.when((c >= 0) & (c < chunks))
+            def _():
+                ring.step(s, c)
+
+        return carry
+
+    lax.fori_loop(0, chunks + LAG * (Ring.STEPS - 1), tick, 0)
+
+    def drain(c, carry):
+        for half in range(2):
+            ring.save(half, c).wait()
+        return carry
+
+    lax.fori_loop(0, chunks, drain, 0)
+
+
+def reduce_grads(grads, number):
+    _, chunks, units, _, lanes = grads.shape
+    lats, lons = lax.axis_size("lat"), lax.axis_size("lon")
+    side = plane_side(lons)
+    sub0 = units // side
+    sub1 = sub0 // side
+    peers = max(side, lats) - 1
+    return pl.pallas_call(
+        functools.partial(reduce_kernel, side, lats),
+        out_shape=jax.ShapeDtypeStruct(grads.shape, BF16),
+        in_specs=[pl.BlockSpec(memory_space=pl.ANY)],
+        out_specs=pl.BlockSpec(memory_space=pl.ANY),
+        scratch_shapes=[
+            pltpu.VMEM((2, chunks, units, 8, lanes), BF16),
+            pltpu.VMEM((2, chunks, units, 8, lanes), BF16),
+            pltpu.VMEM((chunks, units, 8, lanes), BF16),
+            pltpu.VMEM((chunks, units, 8, lanes), BF16),
+            pltpu.VMEM((chunks, side - 1, sub0, 8, lanes), BF16),
+            pltpu.VMEM((chunks, side - 1, sub1, 8, lanes), BF16),
+            pltpu.VMEM((chunks, lats - 1, sub1 // lats, 8, lanes), BF16),
+            pltpu.SemaphoreType.DMA((chunks, 8, peers)),
+            pltpu.SemaphoreType.DMA((chunks, 8, peers)),
+            pltpu.SemaphoreType.DMA((2, 2, chunks)),
+        ],
+        compiler_params=pltpu.CompilerParams(
+            collective_id=number, has_side_effects=True, vmem_limit_bytes=56 * 2**20
+        ),
+        name="reduce_grads",
+    )(grads)
+
+
+def plane_side(lons):
+    return int(round((lons // 2) ** 0.5))
+
+
+def ring_fits(lats, lons):
+    side = plane_side(lons)
+    return side >= 2 and lats >= 2 and 2 * side * side == lons and UNITS % (side * side * lats) == 0
+
+
+def reduce_all(d_w_in_t, d_w_out, d_taps):
+    lats, lons = lax.axis_size("lat"), lax.axis_size("lon")
+    hidden, channels = d_w_out.shape
+    rows = UNITS * 8
+    if not ring_fits(lats, lons):
+        values = (d_w_in_t.astype(F32), d_w_out.astype(F32), d_taps)
+        d_w_in_t, d_w_out, d_taps = lax.psum(values, ("lat", "lon"))
+        return d_w_in_t.T, d_w_out, d_taps
+    total = pl.cdiv(hidden + d_taps.shape[0], rows) * rows
+    low = jnp.pad(d_taps.astype(BF16), ((0, total - hidden - d_taps.shape[0]), (0, 0)))
+    first = jnp.concatenate([d_w_out, low], axis=0)
+    second = jnp.pad(d_w_in_t, ((0, total - hidden), (0, 0)))
+    grads = jnp.stack([first, second]).reshape(2, total // rows, UNITS, 8, channels)
+    done = reduce_grads(grads, 2).reshape(2, total, channels)
+    return (
+        done[1, :hidden].T.astype(F32),
+        done[0, :hidden].astype(F32),
+        done[0, hidden : hidden + d_taps.shape[0]].astype(F32),
+    )
 
 
 def spread_kernel(ker_ref, taps):
@@ -278,7 +509,7 @@
     pre_low = d_pre.astype(BF16)
     local_b_in = jnp.sum(d_pre, axis=0)
     local_w_in = lax.dot_general(
-        normed, pre_low, (((0,), (0,)), ((), ())), preferred_element_type=F32
+        pre_low, normed, (((0,), (0,)), ((), ())), preferred_element_type=F32
     ).astype(BF16)
     d_normed = lax.dot_general(
         pre_low, w_in, (((1,), (1,)), ((), ())), preferred_element_type=F32
@@ -299,17 +530,16 @@
     )
     d_padded = with_halo(d_conv.astype(BF16))
     d_inputs, local_kernel = depthwise_back(padded, d_padded, taps, cotangent, kept_steps)
-    d_w_in, d_w_out = lax.psum((local_w_in, local_w_out), ("lat", "lon"))
-    d_kernel = lax.psum(local_kernel, ("lat", "lon"))
+    d_w_in, d_w_out, d_kernel = reduce_all(local_w_in, local_w_out, local_kernel)
     return (
         output,
         d_inputs,
         d_kernel.reshape(conv_kernel.shape),
         d_gain,
         d_shift,
-        d_w_in.astype(F32),
+        d_w_in,
         d_b_in,
-        d_w_out.astype(F32),
+        d_w_out,
         d_b_out,
     )
 

time: 528 us -> 452 us (0.86)
  waiting for transfers between devices: 266 us -> 24.4 us
  Pallas kernels: 82.4 us -> 204 us
  local copies, waits for them, and re-layouts: 25.4 us -> 73.6 us
  other arithmetic: 43.3 us -> 59.6 us
  between operations: 15.1 us -> 2.02 us
  matrix products: 75.2 us -> 64.4 us
    psum x2 -> x0, waiting for transfers between devices: 222 us -> none  [the longest x1 118 us: body(): d_kernel = lax.psum(local_kernel, ('lat', 'lon'))]
    pallas_call x0 -> x1, Pallas kernels: none -> 124 us  [reduce_grads(): pl.pallas_call(functools.partial(reduce_kernel, side, lats), out_shape=ja...]
    unnamed x47 -> x54, local copies, waits for them, and re-layouts: 5.52 us -> 34 us
    ppermute x4, waiting for transfers between devices: 35 us -> 14.1 us  [with_halo(): before = lax.ppermute(last, axis, up)]
    another operation x0 -> x1, other arithmetic: none -> 10.4 us  [reduce_all(): jnp.stack([first, second]).reshape(2, total // rows, UNITS, 8, channels)]
    slice x0 -> x1, local copies, waits for them, and re-layouts: none -> 9.64 us  [reduce_all(): done[0, :hidden].astype(F32)]
    concatenate x0 -> x1, local copies, waits for them, and re-layouts: none -> 8.88 us  [reduce_all(): first = jnp.concatenate([d_w_out, low], axis=0)]
    pad x0 -> x1, local copies, waits for them, and re-layouts: none -> 5.7 us  [reduce_all(): second = jnp.pad(d_w_in_t, ((0, total - hidden), (0, 0)))]
  transfers between devices with their start and end apart: 10 -> 8, of which waited for: 9 -> 5; matrix products, arithmetic and copies ran while one was open for 9% -> 8% of each run, Pallas kernels for 8% -> 0%
where the time goes in v2:
time: 452 us; the launch traced here: 447 us
  Pallas kernels  204 us (45%)
  local copies, waits for them, and re-layouts  73.6 us (16%)
  matrix products  64.4 us (14%)
  other arithmetic  59.6 us (13%)
  waiting for transfers between devices  24.4 us (5%)
  starting transfers between devices  18.4 us (4%)
    pallas_call x1, Pallas kernels, reduce_grads(): pl.pallas_call(functools.partial(reduce_kernel, side, lats), out_shape=ja...  124 us
    pallas_call x2, Pallas kernels, exchange(): pl.pallas_call(functools.partial(exchange_kernel, merge, sizes), out_shap...  38.6 us
    unnamed x54, local copies, waits for them, and re-layouts  34 us
    pallas_call x1, Pallas kernels, depthwise_back(): pl.pallas_call(backward_kernel, grid=(pl.cdiv(channels, 128),), in_specs=...  27.6 us
    dot_general x1, matrix products, body(): lax.dot_general(branch_low, w_out, (((1,), (1,)), ((), ())), preferred_el...  18.1 us
    pallas_call x1, Pallas kernels, depthwise(): pl.pallas_call(forward_kernel, grid=(pl.cdiv(channels, 128),), in_specs=[...  14.4 us
    ppermute x4, waiting for transfers between devices, with_halo(): before = lax.ppermute(last, axis, up)  14.1 us
    ppermute x4, starting transfers between devices, with_halo(): before = lax.ppermute(last, axis, up)  12.7 us
  transfers between devices with their start and end apart: 8, of which 5 were waited for; matrix products, arithmetic and copies ran while one was open for 8% of the time, Pallas kernels for 0%

profile of v2, /device:TPU:0, one launch (start us, length us, event | category | flops | bytes accessed | tf_op | source)
XLA Modules:
  0.0 446.6 jit_solution(14623410634691686664)
XLA Ops:
  2.3 5.1 %collective-permute-start = (bf16[4,3,32,800]{3,2,1,0:T(8,128)(2,1)S(1)}, bf16[4,3,32,800]{3,2,1,0:T(8,128)(2,1)S(1)}, u32[]{:S(2)}, u32[]{:S(2)}) collective-permute-start(bf16[4,3,32,800]{3,2,1,0:T(8,128)(2,1)S(1)} %get-tuple-element.116), channel_id=1, source_target_pairs={{0,8},{8,16},{16,24},{1,9},{9,17},{17,25},{2,10},{10,18},{18,26},{... | collective-permute-start | bytes 1843208 | tf_op jit(solution)/shard_map/ppermute | solution.py:29
  8.7 13.3 %collective-permute-done = bf16[4,3,32,800]{3,2,1,0:T(8,128)(2,1)S(1)} collective-permute-done((bf16[4,3,32,800]{3,2,1,0:T(8,128)(2,1)S(1)}, bf16[4,3,32,800]{3,2,1,0:T(8,128)(2,1)S(1)}, u32[]{:S(2)}, u32[]{:S(2)}) %collective-permute-start) | collective-permute-done | bytes 614432 | tf_op jit(solution)/shard_map/ppermute | solution.py:29
  22.5 3.7 collective-permute-done.1
  35.2 3.5 pad_maximum_fusion.1.p_ref
  38.7 14.4 %depthwise.1 = f32[4,8,32,800]{3,2,1,0:T(8,128)} custom-call(bf16[4,14,48,800]{3,2,1,0:T(8,128)(2,1)} %pad_maximum_fusion.1.p_ref, bf16[49,800]{1,0:T(8,128)(2,1)} %reshape.252.ker_ref), custom_call_target="tpu_custom_call" | custom-call | tf_op jit(solution)/shard_map/depthwise/pallas_call | solution.py:386
  59.7 27.3 %exchange0.1 = f32[8,800]{1,0:T(8,128)} custom-call(f32[8,800]{1,0:T(8,128)} %copy-done.7), custom_call_target="tpu_custom_call" | custom-call | tf_op jit(solution)/shard_map/exchange0/pallas_call | solution.py:100
  93.7 9.7 %fusion.21 = f32[1024,3200]{1,0:T(8,128)S(1)} fusion(bf16[1024,800]{1,0:T(8,128)(2,1)S(1)} %bitcast.35, bf16[800,3200]{1,0:T(8,128)(2,1)} %param.29), kind=kOutput, calls=%fused_computation.55 | convolution fusion | flops 5242880000 | bytes 19865600 | tf_op jit(solution)/shard_map/dot_general | solution.py:494
  103.4 4.7 %copy-done.19 = f32[1024,3200]{1,0:T(8,128)} copy-done((f32[1024,3200]{1,0:T(8,128)}, f32[1024,3200]{1,0:T(8,128)S(1)}, u32[]{:S(2)}) %copy-start.19) | copy-done | bytes 13107224
  108.1 6.4 %convolution_add_fusion = f32[1024,800]{0,1:T(8,128)S(1)} fusion(bf16[3200,800]{0,1:T(8,128)(2,1)S(1)} %bitcast.38, f32[800]{0:T(1024)S(1)} %convert_element_type.91, f32[1024,3200]{1,0:T(8,128)S(1)} %fusion.21, f32[3200]{0:T(1024)S(1)} %convert_element_type.89), kind=kOutput, calls=%fused_computation.32 | convolution fusion | flops 5276467200 | bytes 21520000 | tf_op jit(solution)/shard_map/dot_general | solution.py:497
  114.5 3.3 copy.27
  117.8 18.1 %fusion.13 = (f32[3200]{0:T(1024)S(1)}, bf16[1024,3200]{1,0:T(8,128)(2,1)}) fusion(f32[1024,3200]{1,0:T(8,128)} %copy-done.19, f32[3200]{0:T(1024)S(1)} %convert_element_type.89, bf16[1024,800]{1,0:T(8,128)(2,1)} %bitcast.33, bf16[3200,800]{0,1:T(8,128)(2,1)} %param.31), kind=kOutput, calls=%fused_computation.48 | convolution fusion | flops 5314966528 | bytes 26444800 | tf_op jit(solution)/shard_map/dot_general | solution.py:507
  136.0 9.6 %fusion.20 = (f32[800]{0:T(1024)S(1)}, f32[1024,800]{0,1:T(8,128)S(1)}) fusion(bf16[800,3200]{1,0:T(8,128)(2,1)} %param.29, bf16[1024,3200]{1,0:T(8,128)(2,1)} %get-tuple-element.105), kind=kOutput, calls=%fused_computation.54 | convolution fusion | flops 5243698176 | bytes 14953600 | tf_op jit(solution)/shard_map/dot_general | solution.py:514
  145.6 3.3 copy.28
  148.9 3.8 multiply_reduce_fusion
  153.7 11.3 %exchange1.1 = f32[8,800]{1,0:T(8,128)} custom-call(f32[8,800]{1,0:T(8,128)} %copy-done.6), custom_call_target="tpu_custom_call" | custom-call | tf_op jit(solution)/shard_map/exchange1/pallas_call | solution.py:100
  166.5 7.4 %multiply_convert_fusion.1 = (bf16[4,8,32,800]{3,2,1,0:T(8,128)(2,1)S(1)}, bf16[4,8,32,800]{3,2,1,0:T(8,128)(2,1)}) fusion(f32[4,8,32,800]{3,2,1,0:T(8,128)} %depthwise.1, f32[]{:T(128)} %bitcast, f32[800]{0:T(1024)S(1)} %get-tuple-element.98, f32[800]{0:T(1024)S(1)} %get-tuple-element.99, f32[800]{0:T(1024)S(1)} %convert_multiply_fusion, ...), kind=kLoop, calls=%fused_computation.19 | loop fusion | flops 10649600 | bytes 14762628 | tf_op jit(solution)/shard_map/convert_element_type | solution.py:531
  174.0 3.1 collective-permute-start.4
  178.8 12.6 %convolution_convert_fusion.1 = bf16[3200,800]{0,1:T(8,128)(2,1)} fusion(bf16[1024,800]{1,0:T(8,128)(2,1)S(1)} %bitcast.34, f32[1024,3200]{1,0:T(8,128)} %copy-done.19, f32[3200]{0:T(1024)S(1)} %convert_element_type.89), kind=kOutput, calls=%fused_computation.14 | convolution fusion | flops 5278208000 | bytes 19878400 | tf_op jit(solution)/shard_map/dot_general | solution.py:504
  192.1 4.6 %collective-permute-done.5 = bf16[4,3,32,800]{3,2,1,0:T(8,128)(2,1)S(1)} collective-permute-done((bf16[4,3,32,800]{3,2,1,0:T(8,128)(2,1)S(1)}, bf16[4,3,32,800]{3,2,1,0:T(8,128)(2,1)S(1)}, u32[]{:S(2)}, u32[]{:S(2)}) %collective-permute-start.5) | collective-permute-done | bytes 614432 | tf_op jit(solution)/shard_map/ppermute | solution.py:30
  201.9 8.1 %convolution_convert_fusion = bf16[3200,800]{0,1:T(8,128)(2,1)} fusion(bf16[1024,800]{1,0:T(8,128)(2,1)S(1)} %bitcast.36, bf16[1024,3200]{1,0:T(8,128)(2,1)S(1)} %bitcast.40), kind=kOutput, calls=%fused_computation.13 | convolution fusion | flops 5245440000 | bytes 13312000 | tf_op jit(solution)/shard_map/dot_general | solution.py:511
  210.0 8.7 %copy.37 = bf16[3200,800]{1,0:T(8,128)(2,1)} copy(bf16[3200,800]{0,1:T(8,128)(2,1)} %convolution_convert_fusion) | data formatting | bytes 10240000
  219.3 5.7 %pad.25.clone = bf16[3328,800]{1,0:T(8,128)(2,1)} pad(bf16[3200,800]{1,0:T(8,128)(2,1)} %copy.37, bf16[]{:T(256)} %constant.195.clone.1), padding=0_128x0_0 | pad | bytes 10444802 | tf_op jit(solution)/shard_map/jit(_pad)/pad | solution.py:338
  225.0 3.5 pad_maximum_fusion.2.d_ref
  228.6 27.6 %depthwise_back.1 = (bf16[4,8,32,800]{3,2,1,0:T(8,128)(2,1)}, f32[49,800]{1,0:T(8,128)}) custom-call(bf16[4,14,48,800]{3,2,1,0:T(8,128)(2,1)} %pad_maximum_fusion.1.p_ref, bf16[4,14,48,800]{3,2,1,0:T(8,128)(2,1)} %pad_maximum_fusion.2.d_ref, bf16[49,800]{1,0:T(8,128)(2,1)} %reshape.252.ker_ref, bf16[4,8,32,800]{3,2,1,0:T(8,128)(2,1)} %g_ref.1, f32[4]{0:T(128)} %copy-done.17), custom_call_target="tpu_custom_call" | custom-call | tf_op jit(solution)/shard_map/depthwise_back/pallas_call | solution.py:441
  257.3 5.2 %fusion.7 = bf16[3328,800]{0,1:T(8,128)(2,1)} fusion(bf16[49,800]{0,1:T(8,128)(2,1)S(1)} %copy.36, bf16[3200,800]{0,1:T(8,128)(2,1)} %convolution_convert_fusion.1), kind=kLoop, calls=%fused_computation.15 | loop fusion | flops 15974400 | bytes 10523200 | tf_op jit(solution)/shard_map/concatenate | solution.py:337
  262.5 8.9 %copy.30 = bf16[3328,800]{1,0:T(8,128)(2,1)} copy(bf16[3328,800]{0,1:T(8,128)(2,1)} %fusion.7) | data formatting | bytes 10649600 | tf_op jit(solution)/shard_map/concatenate | solution.py:337
  271.3 10.4 %pad_maximum_fusion.grads = bf16[2,26,16,8,800]{4,3,2,1,0:T(8,128)(2,1)} fusion(bf16[1,26,16,8,800]{4,3,2,1,0:T(8,128)(2,1)} %bitcast.30, bf16[1,26,16,8,800]{4,3,2,1,0:T(8,128)(2,1)} %bitcast.31), kind=kLoop, calls=%fused_computation.9 | loop fusion | flops 5324800 | bytes 21299200 | tf_op jit(solution)/shard_map/stack | solution.py:339
  281.8 123.5 %reduce_grads.1 = bf16[2,26,16,8,800]{4,3,2,1,0:T(8,128)(2,1)} custom-call(bf16[2,26,16,8,800]{4,3,2,1,0:T(8,128)(2,1)} %pad_maximum_fusion.grads), custom_call_target="tpu_custom_call" | custom-call | tf_op jit(solution)/shard_map/reduce_grads/pallas_call | solution.py:294
  406.3 9.6 %fusion.15 = (bf16[1,3200,800]{2,1,0:T(8,128)(2,1)}, bf16[1,3200,800]{2,1,0:T(8,128)(2,1)}) fusion(bf16[2,3328,800]{2,1,0:T(8,128)(2,1)} %bitcast.29), kind=kLoop, calls=%fused_computation.49 | loop fusion | bytes 20480000 | tf_op jit(solution)/shard_map/slice | solution.py:343
  415.9 8.5 %copy.35 = bf16[1,3200,800]{1,2,0:T(8,128)(2,1)} copy(bf16[1,3200,800]{2,1,0:T(8,128)(2,1)} %get-tuple-element.106) | data formatting | bytes 10240000
  425.1 8.5 %copy.34 = bf16[1,3200,800]{1,2,0:T(8,128)(2,1)} copy(bf16[1,3200,800]{2,1,0:T(8,128)(2,1)} %get-tuple-element.107) | data formatting | bytes 10240000
  433.7 12.7 %convert_bitcast_fusion = (f32[800,3200]{1,0:T(8,128)}, f32[3200,800]{0,1:T(8,128)}) fusion(bf16[1,3200,800]{1,2,0:T(8,128)(2,1)} %copy.34, bf16[1,3200,800]{1,2,0:T(8,128)(2,1)} %copy.35), kind=kLoop, calls=%fused_computation.12 | loop fusion | flops 5120000 | bytes 30720000 | tf_op jit(solution)/shard_map/convert_element_type | solution.py:342
  (102 shorter events, 38.3 us)
Async XLA Ops:
  0.6 21.5 %copy-start.1 = (bf16[4,8,32,800]{3,2,1,0:T(8,128)(2,1)S(1)}, bf16[4,8,32,800]{3,2,1,0:T(8,128)(2,1)}, u32[]{:S(2)}) copy-start(bf16[4,8,32,800]{3,2,1,0:T(8,128)(2,1)} %param.25) | copy-start | bytes 4915204
  2.2 28.9 %copy-start.15 = (bf16[800]{0:T(1024)(128)(2,1)S(1)}, bf16[800]{0:T(1024)(128)(2,1)}, u32[]{:S(2)}) copy-start(bf16[800]{0:T(1024)(128)(2,1)} %param.28) | copy-start | bytes 4804
  2.2 28.9 %copy-start.16 = (bf16[800]{0:T(1024)(128)(2,1)S(1)}, bf16[800]{0:T(1024)(128)(2,1)}, u32[]{:S(2)}) copy-start(bf16[800]{0:T(1024)(128)(2,1)} %param.32) | copy-start | bytes 4804
  2.2 28.9 %copy-start.13 = (bf16[800]{0:T(1024)(128)(2,1)S(1)}, bf16[800]{0:T(1024)(128)(2,1)}, u32[]{:S(2)}) copy-start(bf16[800]{0:T(1024)(128)(2,1)} %param.27) | copy-start | bytes 4804
  2.2 28.9 %copy-start.14 = (s32[8,32]{1,0:T(8,128)S(1)}, s32[8,32]{1,0:T(8,128)}, u32[]{:S(2)}) copy-start(s32[8,32]{1,0:T(8,128)} %param.33) | copy-start | bytes 3076
  2.3 30.2 %copy-start.12 = (bf16[3200]{0:T(1024)(128)(2,1)S(1)}, bf16[3200]{0:T(1024)(128)(2,1)}, u32[]{:S(2)}) copy-start(bf16[3200]{0:T(1024)(128)(2,1)} %param.30) | copy-start | bytes 19204
  2.3 30.2 %copy-start.9 = (bf16[7,7,800]{2,1,0:T(8,128)(2,1)S(1)}, bf16[7,7,800]{2,1,0:T(8,128)(2,1)}, u32[]{:S(2)}) copy-start(bf16[7,7,800]{2,1,0:T(8,128)(2,1)} %param.26) | copy-start | bytes 235204
  2.3 30.9 %copy-start.18 = (s32[4]{0:T(128)S(1)}, s32[4]{0:T(128)}, u32[]{:S(2)}) copy-start(s32[4]{0:T(128)} %param.34) | copy-start | bytes 52
  2.3 19.8 %collective-permute-start = (bf16[4,3,32,800]{3,2,1,0:T(8,128)(2,1)S(1)}, bf16[4,3,32,800]{3,2,1,0:T(8,128)(2,1)S(1)}, u32[]{:S(2)}, u32[]{:S(2)}) collective-permute-start(bf16[4,3,32,800]{3,2,1,0:T(8,128)(2,1)S(1)} %get-tuple-element.116), channel_id=1, source_target_pairs={{0,8},{8,16},{16,24},{1,9},{9,17},{17,25},{2,10},{10,18},{18,26},{... | collective-permute-start | bytes 1843208 | tf_op jit(solution)/shard_map/ppermute | solution.py:29
  7.4 18.8 %collective-permute-start.1 = (bf16[4,3,32,800]{3,2,1,0:T(8,128)(2,1)S(1)}, bf16[4,3,32,800]{3,2,1,0:T(8,128)(2,1)S(1)}, u32[]{:S(2)}, u32[]{:S(2)}) collective-permute-start(bf16[4,3,32,800]{3,2,1,0:T(8,128)(2,1)S(1)} %get-tuple-element.115), channel_id=1, source_target_pairs={{8,0},{16,8},{24,16},{9,1},{17,9},{25,17},{10,2},{18,10},{26,18},{... | collective-permute-start | bytes 1843208 | tf_op jit(solution)/shard_map/ppermute | solution.py:30
  27.6 5.6 %collective-permute-start.2 = (bf16[4,14,8,800]{3,2,1,0:T(8,128)(2,1)}, bf16[4,14,8,800]{3,2,1,0:T(8,128)(2,1)}, u32[]{:S(2)}, u32[]{:S(2)}) collective-permute-start(bf16[4,14,8,800]{3,2,1,0:T(8,128)(2,1)} %get-tuple-element.110), channel_id=1, source_target_pairs={{0,1},{1,2},{2,3},{3,4},{4,5},{5,6},{6,7},{8,9},{9,10},{10,11},{11... | collective-permute-start | bytes 2150408 | tf_op jit(solution)/shard_map/ppermute | solution.py:29
  29.8 5.3 %collective-permute-start.3 = (bf16[4,14,8,800]{3,2,1,0:T(8,128)(2,1)}, bf16[4,14,8,800]{3,2,1,0:T(8,128)(2,1)}, u32[]{:S(2)}, u32[]{:S(2)}) collective-permute-start(bf16[4,14,8,800]{3,2,1,0:T(8,128)(2,1)} %get-tuple-element.111), channel_id=1, source_target_pairs={{1,0},{2,1},{3,2},{4,3},{5,4},{6,5},{7,6},{9,8},{10,9},{11,10},{12... | collective-permute-start | bytes 2150408 | tf_op jit(solution)/shard_map/ppermute | solution.py:30
  33.2 22.6 %copy-start.17 = (f32[4]{0:T(128)}, f32[4]{0:T(128)S(1)}, u32[]{:S(2)}) copy-start(f32[4]{0:T(128)S(1)} %convert_multiply_fusion.1.share_ref) | copy-start | bytes 52
  38.7 17.1 %copy-start.2 = (bf16[4,8,32,800]{3,2,1,0:T(8,128)(2,1)S(1)}, bf16[4,8,32,800]{3,2,1,0:T(8,128)(2,1)}, u32[]{:S(2)}) copy-start(bf16[4,8,32,800]{3,2,1,0:T(8,128)(2,1)} %g_ref.1) | copy-start | bytes 4915204
  53.1 3.1 copy-start
  59.0 0.6 copy-start.7
  89.7 18.5 %slice-start = ((s8[5120000]{0:T(1024)(128)(4,1)}), s8[4194304]{0:T(1024)(128)(4,1)S(1)}, s32[]{:S(2)}) async-start(s8[5120000]{0:T(1024)(128)(4,1)} %bitcast.37), calls=%async_computation | async-start | bytes 8388608
  92.5 1.2 copy-start.4
  93.7 14.4 %slice-start.1 = ((s8[5120000]{0:T(1024)(128)(4,1)}), s8[925696]{0:T(1024)(128)(4,1)S(1)}, s32[]{:S(2)}) async-start(s8[5120000]{0:T(1024)(128)(4,1)} %bitcast.37), calls=%async_computation.1 | async-start | bytes 1851392
  103.4 4.7 %copy-start.19 = (f32[1024,3200]{1,0:T(8,128)}, f32[1024,3200]{1,0:T(8,128)S(1)}, u32[]{:S(2)}) copy-start(f32[1024,3200]{1,0:T(8,128)S(1)} %fusion.21) | copy-start | bytes 39321604
  153.1 0.6 copy-start.6
  166.5 7.4 %copy-start.10 = (f32[800]{0:T(1024)}, f32[800]{0:T(1024)S(1)}, u32[]{:S(2)}) copy-start(f32[800]{0:T(1024)S(1)} %get-tuple-element.98) | copy-start | bytes 9604
  166.5 7.4 %copy-start.11 = (f32[800]{0:T(1024)}, f32[800]{0:T(1024)S(1)}, u32[]{:S(2)}) copy-start(f32[800]{0:T(1024)S(1)} %get-tuple-element.99) | copy-start | bytes 9604
  166.5 12.2 %copy-start.3 = (bf16[4,8,32,800]{3,2,1,0:T(8,128)(2,1)S(1)}, bf16[4,8,32,800]{3,2,1,0:T(8,128)(2,1)}, u32[]{:S(2)}) copy-start(bf16[4,8,32,800]{3,2,1,0:T(8,128)(2,1)} %get-tuple-element.112) | copy-start | bytes 4915204
  174.0 18.1 %collective-permute-start.4 = (bf16[4,3,32,800]{3,2,1,0:T(8,128)(2,1)S(1)}, bf16[4,3,32,800]{3,2,1,0:T(8,128)(2,1)S(1)}, u32[]{:S(2)}, u32[]{:S(2)}) collective-permute-start(bf16[4,3,32,800]{3,2,1,0:T(8,128)(2,1)S(1)} %get-tuple-element.113), channel_id=1, source_target_pairs={{0,8},{8,16},{16,24},{1,9},{9,17},{17,25},{2,10},{10,18},{18,26},{... | collective-permute-start | bytes 1843208 | tf_op jit(solution)/shard_map/ppermute | solution.py:29
  177.1 24.7 %slice-start.2 = ((s8[6553600]{0:T(1024)(128)(4,1)}), s8[4194304]{0:T(1024)(128)(4,1)S(1)}, s32[]{:S(2)}) async-start(s8[6553600]{0:T(1024)(128)(4,1)} %bitcast.39), calls=%async_computation.2 | async-start | bytes 8388608
  177.2 24.7 %copy-start.5 = (bf16[4,8,32,800]{3,2,1,0:T(8,128)(2,1)S(1)}, bf16[4,8,32,800]{3,2,1,0:T(8,128)(2,1)}, u32[]{:S(2)}) copy-start(bf16[4,8,32,800]{3,2,1,0:T(8,128)(2,1)} %copy-done.4) | copy-start | bytes 4915204
  177.2 24.7 %slice-start.3 = ((s8[6553600]{0:T(1024)(128)(4,1)}), s8[2359296]{0:T(1024)(128)(4,1)S(1)}, s32[]{:S(2)}) async-start(s8[6553600]{0:T(1024)(128)(4,1)} %bitcast.39), calls=%async_computation.3 | async-start | bytes 4718592
  177.2 19.5 %collective-permute-start.5 = (bf16[4,3,32,800]{3,2,1,0:T(8,128)(2,1)S(1)}, bf16[4,3,32,800]{3,2,1,0:T(8,128)(2,1)S(1)}, u32[]{:S(2)}, u32[]{:S(2)}) collective-permute-start(bf16[4,3,32,800]{3,2,1,0:T(8,128)(2,1)S(1)} %get-tuple-element.114), channel_id=1, source_target_pairs={{8,0},{16,8},{24,16},{9,1},{17,9},{25,17},{10,2},{18,10},{26,18},{... | collective-permute-start | bytes 1843208 | tf_op jit(solution)/shard_map/ppermute | solution.py:30
  198.0 27.0 %collective-permute-start.6 = (bf16[4,14,8,800]{3,2,1,0:T(8,128)(2,1)}, bf16[4,14,8,800]{3,2,1,0:T(8,128)(2,1)}, u32[]{:S(2)}, u32[]{:S(2)}) collective-permute-start(bf16[4,14,8,800]{3,2,1,0:T(8,128)(2,1)} %get-tuple-element.108), channel_id=1, source_target_pairs={{0,1},{1,2},{2,3},{3,4},{4,5},{5,6},{6,7},{8,9},{9,10},{10,11},{11... | collective-permute-start | bytes 2150408 | tf_op jit(solution)/shard_map/ppermute | solution.py:29
  200.2 9.7 %copy-start.8 = (f32[8,800]{1,0:T(8,128)S(1)}, f32[8,800]{1,0:T(8,128)}, u32[]{:S(2)}) copy-start(f32[8,800]{1,0:T(8,128)} %exchange1.1) | copy-start | bytes 76804
  200.2 24.8 %collective-permute-start.7 = (bf16[4,14,8,800]{3,2,1,0:T(8,128)(2,1)}, bf16[4,14,8,800]{3,2,1,0:T(8,128)(2,1)}, u32[]{:S(2)}, u32[]{:S(2)}) collective-permute-start(bf16[4,14,8,800]{3,2,1,0:T(8,128)(2,1)} %get-tuple-element.109), channel_id=1, source_target_pairs={{1,0},{2,1},{3,2},{4,3},{5,4},{6,5},{7,6},{9,8},{10,9},{11,10},{12... | collective-permute-start | bytes 2150408 | tf_op jit(solution)/shard_map/ppermute | solution.py:30
